TPU v7x, 256 devices: a 2x2x32 block of a 4x8x32 slice. The times are simulated.
256 devices in a mesh: scen: 4 (over x, y), lon: 64 (over z, core).
Axes of the slice: x: 2, y: 2, z: 32, core: 2. Of those that a mesh axis runs over, the one named last changes fastest.
The devices are a block of a 4x8x32 slice.
Arguments:
- tracer: float32 [32, 4, 2048, 1024], P('scen', None, 'lon'), parts along dimension 0, may hold values from 0.25 to 15, as said below
- offsets: int32 [4, 2048, 1024], P(None, 'lon'), may hold values from -12 to 12
- frac: float32 [4, 1024], replicated, may hold values from 0.02 to 0.98
- air_before: float32 [4, 2048, 1024], P(None, 'lon'), may hold values from 0.5 to 2
- air_after: float32 [4, 2048, 1024], P(None, 'lon'), may hold values from 0.05 to 15, as said below
- growth: float32 [32], P('scen'), parts along dimension 0, may hold values from 0.05 to 0.5
Outputs:
- tracer_next: float32 [32, 4, 2048, 1024], P('scen', None, 'lon'), parts along dimension 0
There are 4 independent parts, one for each index of `scen`. A program takes and returns all parts, laid end to end along the dimension named above; an argument that names none is the same for every part. Nothing has to cross between parts.
Inputs may be any that keep to these rules, and one draw needn't show every extreme that they name: `tracer`: positive mixing ratios. `air_after`: positive air masses.
All inputs are finite; a program needn't handle non-finite values.
Results may differ from a plain program's by a relative error of at most 0.00002.
Values sent between devices are 32-bit elements; how exact they have to be, the bound alone decides.
A program may use at most 64 MiB of HBM per device.

v0:
```python
import jax
import jax.numpy as jnp
from jax import lax
from jax.sharding import PartitionSpec as P

OFFMAX = 12


def with_halo(block, sides, width):
    for axis, dim in sides:
        count = lax.axis_size(axis)
        forward = [(i, i + 1) for i in range(count - 1)]
        forward.append((count - 1, 0))
        backward = [(target, source) for source, target in forward]
        low = lax.ppermute(
            lax.slice_in_dim(block, block.shape[dim] - width, None, axis=dim), axis, forward
        )
        high = lax.ppermute(lax.slice_in_dim(block, 0, width, axis=dim), axis, backward)
        block = jnp.concatenate([low, block, high], axis=dim)
    return block


def from_everyone(array, axis):
    copies = jnp.broadcast_to(array, (lax.axis_size(axis), *array.shape))
    return lax.all_to_all(copies, axis, split_axis=0, concat_axis=0, tiled=True)


def taken_together(array, axis):
    return from_everyone(array, axis).sum(axis=0)


def packed_total(arrays, axis):
    flat, at, done = (jnp.concatenate([a.reshape(-1) for a in arrays]), 0, [])
    so_far = taken_together(flat, axis)
    for a in arrays:
        done.append(so_far[at : at + a.size].reshape(a.shape))
        at += a.size
    return tuple(done)


def cubic_weights(fraction):
    first = -fraction * (1.0 - fraction) * (2.0 - fraction) / 6.0
    second = (1.0 + fraction) * (1.0 - fraction) * (2.0 - fraction) / 2.0
    third = (1.0 + fraction) * fraction * (2.0 - fraction) / 2.0
    fourth = -(1.0 + fraction) * fraction * (1.0 - fraction) / 6.0
    return (first, second, third, fourth)


def limited_values(padded, offsets, weights, margin, furthest):
    span_cols = offsets.shape[1]
    lon_dim = padded.ndim - 2
    empty = jnp.zeros(padded.shape[:-2] + (span_cols, padded.shape[-1]), jnp.float32)
    stencil = [empty, empty, empty, empty]
    for offset_value in range(-furthest, furthest + 1):
        chosen = offsets == offset_value
        for offset_tap in range(4):
            begin_at = margin - offset_value - 1 + offset_tap
            window = lax.slice_in_dim(padded, begin_at, begin_at + span_cols, axis=lon_dim)
            stencil[offset_tap] = jnp.where(chosen, window, stencil[offset_tap])
    cubic = weights[0] * stencil[0] + weights[1] * stencil[1]
    cubic = cubic + weights[2] * stencil[2] + weights[3] * stencil[3]
    lower_bound = jnp.minimum(stencil[1], stencil[2])
    upper_bound = jnp.maximum(stencil[1], stencil[2])
    return jnp.clip(cubic, lower_bound, upper_bound)


def on_device(tracer, offsets, frac, air_before, air_after, growth):
    margin = OFFMAX + 2
    weights = tuple((item[:, None, :] for item in cubic_weights(frac)))
    before_local = jnp.sum(tracer * air_before[None], axis=(1, 2, 3))
    padded = with_halo(tracer, (("lon", 2),), margin)
    limited = limited_values(padded, offsets, weights, margin, OFFMAX)
    after_local = jnp.sum(limited * air_after[None], axis=(1, 2, 3))
    before_total, after_total = packed_total((before_local, after_local), "lon")
    factor = before_total * (1.0 + growth) / after_total
    return limited * factor[:, None, None, None]


def solution(mesh):
    placed = (
        P("scen", None, "lon", None),
        P(None, "lon", None),
        P(),
        P(None, "lon", None),
        P(None, "lon", None),
        P("scen"),
    )
    return jax.shard_map(
        on_device,
        mesh=mesh,
        in_specs=placed,
        out_specs=P("scen", None, "lon", None),
        check_vma=False,
    )
```

profile of v0, /device:TPU:37, one launch (start us, length us, event | category | flops | bytes accessed | tf_op | source)
XLA Modules:
  0.0 140.5 jit_solution(11340835995961895685)
XLA Ops:
  0.0 3.0 %fusion.51 = (f32[8,4,14,1024]{3,2,1,0:T(8,128)S(1)}, f32[8,4,14,1024]{3,2,1,0:T(8,128)S(1)}) fusion(f32[8,4,32,1024]{3,2,1,0:T(8,128)} %param.6), kind=kLoop, calls=%fused_computation.112 | loop fusion | bytes 7340032 | tf_op jit(solution)/shard_map/slice | solution.py:16
  3.0 0.0 copy-start.4
  3.0 0.0 copy-start
  3.0 0.0 copy-start.2
  3.0 1.1 copy.21
  4.1 3.2 %collective-permute-start = (f32[8,4,14,1024]{3,0,2,1:T(8,128)S(1)}, f32[8,4,14,1024]{3,0,2,1:T(8,128)S(1)}, u32[]{:S(2)}, u32[]{:S(2)}) collective-permute-start(f32[8,4,14,1024]{3,0,2,1:T(8,128)S(1)} %copy.21), channel_id=1, source_target_pairs={{0,1},{1,2},{2,3},{3,4},{4,5},{5,6},{6,7},{7,8},{8,9},{9,10},{10,1... | collective-permute-start | bytes 5505032 | tf_op jit(solution)/shard_map/ppermute | solution.py:15
  7.3 1.1 copy.22
  8.4 17.3 %collective-permute-start.1 = (f32[8,4,14,1024]{3,0,2,1:T(8,128)S(1)}, f32[8,4,14,1024]{3,0,2,1:T(8,128)S(1)}, u32[]{:S(2)}, u32[]{:S(2)}) collective-permute-start(f32[8,4,14,1024]{3,0,2,1:T(8,128)S(1)} %copy.22), channel_id=1, source_target_pairs={{1,0},{2,1},{3,2},{4,3},{5,4},{6,5},{7,6},{8,7},{9,8},{10,9},{11,1... | collective-permute-start | bytes 5505032 | tf_op jit(solution)/shard_map/ppermute | solution.py:18
  25.7 0.0 copy-done.4
  25.7 0.0 copy-done
  25.7 0.0 copy-done.2
  25.7 0.0 copy-start.3
  25.8 1.6 %multiply_reduce_fusion.1 = (f32[8]{0:T(128)}, f32[8,4,46,1024]{3,2,1,0:T(8,128)S(1)}) fusion(f32[8,4,32,1024]{3,2,1,0:T(8,128)S(1)} %copy-done, f32[4,32,1024]{2,1,0:T(8,128)S(1)} %copy-done.2), kind=kLoop, calls=%fused_computation.70 | loop fusion | flops 2097143 | bytes 8912928 | tf_op jit(solution)/shard_map/reduce_sum | solution.py:70
  27.4 0.0 copy-done.3
  27.4 2.9 %broadcast_compare_fusion.24 = (pred[4,32,1024]{2,1,0:T(8,128)(4,1)S(1)}, pred[4,32,1024]{2,1,0:T(8,128)(4,1)S(1)}, pred[4,32,1024]{2,1,0:T(8,128)(4,1)S(1)}, pr...) fusion(s32[4,32,1024]{2,1,0:T(8,128)S(1)} %copy-done.3), kind=kLoop, calls=%fused_computation.97 | loop fusion | flops 3276800 | bytes 3801088 | tf_op jit(solution)/shard_map/eq | solution.py:55
  30.3 0.0 copy-start.1
  30.3 0.0 collective-permute-done
  30.3 1.1 copy.16
  31.4 0.0 collective-permute-done.1
  31.4 1.1 copy_dynamic-update-slice_fusion
  32.5 0.0 copy-done.1
  32.5 47.3 %multiply_reduce_fusion = (f32[8]{0:T(128)S(1)}, f32[8,4,32,1024]{3,2,1,0:T(8,128)}) fusion(f32[4,32,1024]{2,1,0:T(8,128)S(1)} %copy-done.1, f32[8,4,32,1024]{3,2,1,0:T(8,128)} %param.6, f32[8,4,46,1024]{3,2,1,0:T(8,128)S(1)} %copy_dynamic-update-slice_fusion, f32[4,1024]{1,0:T(4,128)S(1)} %get-tuple-element.38, f32[4,1024]{1,0:T(4,128)S(1)} %get-tuple-element.39, ...), kind=kLoop, calls=%fused_computation.69 | loop fusion | flops 132120568 | bytes 72810528 | tf_op jit(solution)/shard_map/reduce_sum | solution.py:73
  79.8 0.7 pad_maximum_fusion.1
  80.6 54.0 %all_to_all.6 = f32[64,1,16]{2,1,0:T(1,128)S(1)} all-to-all(f32[64,1,16]{2,1,0:T(1,128)S(1)} %broadcast_in_dim.186), channel_id=1, replica_groups=mesh['scen'=4,'lon'=64] {'lon'}, dimensions={0} | all-to-all | bytes 8192 | tf_op jit(solution)/shard_map/all_to_all | solution.py:25
  134.6 0.1 reduce_sum.29
  134.7 0.7 slice_divide_fusion
  135.4 5.1 %broadcast_multiply_fusion = f32[8,4,32,1024]{3,2,1,0:T(8,128)} fusion(f32[8,4,32,1024]{3,2,1,0:T(8,128)} %get-tuple-element.6, f32[8]{0:T(128)S(1)} %slice_divide_fusion), kind=kLoop, calls=%fused_computation.72 | loop fusion | flops 1048576 | bytes 8388640 | tf_op jit(solution)/shard_map/mul | solution.py:76
  (2 shorter events, 0.0 us)
Async XLA Ops:
  3.0 22.7 %copy-start.4 = (f32[4,1024]{1,0:T(4,128)S(1)}, f32[4,1024]{1,0:T(4,128)}, u32[]{:S(2)}) copy-start(f32[4,1024]{1,0:T(4,128)} %param.8) | copy-start | bytes 49156
  3.0 22.7 %copy-start = (f32[8,4,32,1024]{3,2,1,0:T(8,128)S(1)}, f32[8,4,32,1024]{3,2,1,0:T(8,128)}, u32[]{:S(2)}) copy-start(f32[8,4,32,1024]{3,2,1,0:T(8,128)} %param.6) | copy-start | bytes 12582916
  3.0 22.7 %copy-start.2 = (f32[4,32,1024]{2,1,0:T(8,128)S(1)}, f32[4,32,1024]{2,1,0:T(8,128)}, u32[]{:S(2)}) copy-start(f32[4,32,1024]{2,1,0:T(8,128)} %param.9) | copy-start | bytes 1572868
  4.1 26.2 %collective-permute-start = (f32[8,4,14,1024]{3,0,2,1:T(8,128)S(1)}, f32[8,4,14,1024]{3,0,2,1:T(8,128)S(1)}, u32[]{:S(2)}, u32[]{:S(2)}) collective-permute-start(f32[8,4,14,1024]{3,0,2,1:T(8,128)S(1)} %copy.21), channel_id=1, source_target_pairs={{0,1},{1,2},{2,3},{3,4},{4,5},{5,6},{6,7},{7,8},{8,9},{9,10},{10,1... | collective-permute-start | bytes 5505032 | tf_op jit(solution)/shard_map/ppermute | solution.py:15
  8.4 23.1 %collective-permute-start.1 = (f32[8,4,14,1024]{3,0,2,1:T(8,128)S(1)}, f32[8,4,14,1024]{3,0,2,1:T(8,128)S(1)}, u32[]{:S(2)}, u32[]{:S(2)}) collective-permute-start(f32[8,4,14,1024]{3,0,2,1:T(8,128)S(1)} %copy.22), channel_id=1, source_target_pairs={{1,0},{2,1},{3,2},{4,3},{5,4},{6,5},{7,6},{8,7},{9,8},{10,9},{11,1... | collective-permute-start | bytes 5505032 | tf_op jit(solution)/shard_map/ppermute | solution.py:18
  25.7 1.7 %copy-start.3 = (s32[4,32,1024]{2,1,0:T(8,128)S(1)}, s32[4,32,1024]{2,1,0:T(8,128)}, u32[]{:S(2)}) copy-start(s32[4,32,1024]{2,1,0:T(8,128)} %param.7) | copy-start | bytes 1572868
  30.3 2.2 %copy-start.1 = (f32[4,32,1024]{2,1,0:T(8,128)S(1)}, f32[4,32,1024]{2,1,0:T(8,128)}, u32[]{:S(2)}) copy-start(f32[4,32,1024]{2,1,0:T(8,128)} %param.10) | copy-start | bytes 1572868
where the time goes:
time: 141 us
  other arithmetic  58.5 us (41%)
  blocking collectives  54 us (38%)
  starting transfers between devices  20.5 us (15%)
  local copies, waits for them, and re-layouts  7.32 us (5%)
    all_to_all x1, blocking collectives, from_everyone(): return lax.all_to_all(copies, axis, split_axis=0, concat_axis=0, tiled=True)  54 us
    reduce_sum x1, other arithmetic, on_device(): after_local = jnp.sum(limited * air_after[None], axis=(1, 2, 3))  47.3 us
    ppermute x1, starting transfers between devices, with_halo(): lax.ppermute(lax.slice_in_dim(block, 0, width, axis=dim), axis, backward)  17.3 us
    mul x1, other arithmetic, on_device(): return limited * factor[:, None, None, None]  5.11 us
    ppermute x1, starting transfers between devices, with_halo(): lax.ppermute(lax.slice_in_dim(block, block.shape[dim] - width, None, axis...  3.2 us
    slice x1, local copies, waits for them, and re-layouts, with_halo(): lax.slice_in_dim(block, block.shape[dim] - width, None, axis=dim)  2.98 us
    eq x1, other arithmetic, limited_values(): chosen = offsets == offset_value  2.91 us
  transfers between devices with their start and end apart: 2, of which 0 were waited for; matrix products, arithmetic and copies ran while one was open for 5% of the time, Pallas kernels for 0%

commit v1 on v0

v1 whole, which is shorter than its diff:
```python
import functools

import jax
import jax.numpy as jnp
from jax import lax
from jax.experimental import pallas as pl
from jax.experimental.pallas import tpu as pltpu
from jax.sharding import PartitionSpec as P

OFFMAX = 12
LANES = 128
ROWS = 8
LOW = OFFMAX + 1
HIGH = OFFMAX + 2
MESH = pl.DeviceIdType.MESH


def cubic_weights(fraction):
    first = -fraction * (1.0 - fraction) * (2.0 - fraction) / 6.0
    second = (1.0 + fraction) * (1.0 - fraction) * (2.0 - fraction) / 2.0
    third = (1.0 + fraction) * fraction * (2.0 - fraction) / 2.0
    fourth = -(1.0 + fraction) * fraction * (1.0 - fraction) / 6.0
    return (first, second, third, fourth)


def pick(bits, items):
    for bit in bits:
        merged = [jnp.where(bit, items[j + 1], items[j]) for j in range(0, len(items) - 1, 2)]
        if len(items) % 2:
            merged.append(items[-1])
        items = merged
    return items[0]


def kernel(
    dims,
    tracer,
    offsets,
    air_before,
    air_after,
    frac,
    growth,
    out,
    t_in,
    off_in,
    ab_in,
    aa_in,
    t_col,
    k_col,
    ab_col,
    aa_col,
    g_col,
    g_out,
    g_halo,
    f_col,
    weight,
    acc,
    factor,
    row_own,
    row_pair,
    rows_near,
    row_far_out,
    row_far,
    row_side,
    row_other,
    in_sem,
    small_in_sem,
    out_sem,
    edge_send,
    edge_recv,
    g_send,
    g_recv,
    bulk_send,
    bulk_recv,
    know,
    pair_send,
    pair_recv,
    near_send,
    near_recv,
    far_send,
    far_recv,
):
    S, L, W, n = dims
    blocks = W // ROWS
    reach = n // 8
    me = lax.axis_index("lon")
    core = lax.rem(me, 2)
    left, right = lax.rem(me + n - 1, n), lax.rem(me + 1, n)
    partner = me + 1 - 2 * core

    def away(distance):
        return lax.rem(me + distance + n, n)

    barrier = pltpu.get_barrier_semaphore()
    for to in (left, right):
        pl.semaphore_signal(barrier, inc=1, device_id={"lon": to}, device_id_type=MESH)

    load_off = pltpu.make_async_copy(offsets, off_in, small_in_sem.at[0])
    load_aa = pltpu.make_async_copy(air_after, aa_in, small_in_sem.at[1])
    load_ab = pltpu.make_async_copy(air_before, ab_in, small_in_sem.at[2])
    load_off.start()
    load_aa.start()
    load_ab.start()
    for s in range(S):
        pltpu.make_async_copy(tracer.at[s], t_in.at[s], in_sem.at[s]).start()

    def remote(src, dst, send, recv, to):
        return pltpu.make_async_remote_copy(
            src_ref=src, dst_ref=dst, send_sem=send, recv_sem=recv, device_id={"lon": to}, device_id_type=MESH
        )

    edge_up = remote(
        t_col.at[:, :, pl.ds(LOW + W - 1, 1)], t_col.at[:, :, pl.ds(LOW - 1, 1)], edge_send.at[0], edge_recv.at[0], right
    )
    edge_down = remote(
        t_col.at[:, :, pl.ds(LOW, 2)], t_col.at[:, :, pl.ds(LOW + W, 2)], edge_send.at[1], edge_recv.at[1], left
    )
    g_down = remote(g_out.at[0], g_halo.at[1], g_send.at[0], g_recv.at[0], left)
    g_up = remote(g_out.at[1], g_halo.at[0], g_send.at[1], g_recv.at[1], right)

    def bulk_up(s):
        return remote(
            t_col.at[s, :, pl.ds(W, OFFMAX)], t_col.at[s, :, pl.ds(0, OFFMAX)], bulk_send.at[0, s], bulk_recv.at[0, s], right
        )

    def bulk_down(s):
        return remote(
            t_col.at[s, :, pl.ds(LOW + 2, OFFMAX)],
            t_col.at[s, :, pl.ds(LOW + W + 2, OFFMAX)],
            bulk_send.at[1, s],
            bulk_recv.at[1, s],
            left,
        )

    rounds = know.shape[0]

    def tell(r):
        if r >= rounds:
            return
        for side, distance in ((0, 2**r), (1, -(2**r))):
            pl.semaphore_signal(know.at[r, side], inc=1, device_id={"lon": away(distance)}, device_id_type=MESH)

    def hear(r):
        if r >= rounds:
            return
        for side in range(2):
            pl.semaphore_wait(know.at[r, side], 1)

    load_off.wait()
    load_aa.wait()

    def relay_small(x, _):
        lev, blk = x // blocks, lax.rem(x, blocks)
        for l in range(ROWS):
            k_col[lev, blk * ROWS + l] = OFFMAX - off_in[lev, blk, pl.ds(l, ROWS, stride=ROWS), :]
            aa_col[lev, blk * ROWS + l] = aa_in[lev, blk, pl.ds(l, ROWS, stride=ROWS), :]
        return 0

    lax.fori_loop(0, L * blocks, relay_small, 0)

    def weight_of(lev, b):
        total = None
        for i in range(max(0, b - OFFMAX), min(W - 1, b + OFFMAX) + 1):
            term = jnp.where(k_col[lev, i] == OFFMAX - i + b, aa_col[lev, i], 0.0)
            total = term if total is None else total + term
        return total

    def g_sides(lev, _):
        for j in range(OFFMAX):
            g_out[0, lev, j] = weight_of(lev, j - OFFMAX)
            g_out[1, lev, j] = weight_of(lev, W + j)
        return 0

    lax.fori_loop(0, L, g_sides, 0)

    for lev in range(L):
        for j in range(ROWS):
            weight[0, lev, j : j + 1, :] = frac[lev : lev + 1, j * LANES : (j + 1) * LANES]
        for tap, w in enumerate(cubic_weights(weight[0, lev])):
            weight[tap, lev] = w

    pl.semaphore_wait(barrier, 2)
    g_down.start()
    g_up.start()
    tell(0)

    load_ab.wait()

    def relay_before(x, _):
        lev, blk = x // blocks, lax.rem(x, blocks)
        for l in range(ROWS):
            ab_col[lev, blk * ROWS + l] = ab_in[lev, blk, pl.ds(l, ROWS, stride=ROWS), :]
        return 0

    lax.fori_loop(0, L * blocks, relay_before, 0)

    def relay_species(s, _):
        pltpu.make_async_copy(tracer.at[s], t_in.at[s], in_sem.at[s]).wait()

        def relay(x, totals):
            lev, blk = x // blocks, lax.rem(x, blocks)
            totals = list(totals)
            for l in range(ROWS):
                value = t_in[s, lev, blk, pl.ds(l, ROWS, stride=ROWS), :]
                t_col[s, lev, LOW + blk * ROWS + l] = value
                totals[l % 4] = totals[l % 4] + value * ab_col[lev, blk * ROWS + l]
            return tuple(totals)

        zero = jnp.zeros((ROWS, LANES), jnp.float32)
        totals = lax.fori_loop(0, L * blocks, relay, (zero,) * 4)
        acc[s] = (totals[0] + totals[1]) + (totals[2] + totals[3])
        return 0

    lax.fori_loop(0, S, relay_species, 0)
    hear(0)
    tell(1)
    edge_up.start()
    edge_down.start()

    def send_bulk(s, _):
        bulk_up(s).start()
        bulk_down(s).start()
        return 0

    lax.fori_loop(0, S, send_bulk, 0)

    def g_inside(lev, _):
        for b in range(W):
            g_col[lev, b] = weight_of(lev, b)
        return 0

    lax.fori_loop(0, L, g_inside, 0)
    hear(1)
    tell(2)

    def departures(s, lev, first, count):
        w = [weight[tap, lev] for tap in range(4)]
        t = [t_col[s, lev, LOW + first - 1 + j] for j in range(count + 3)]
        for j in range(count):
            cubic = w[0] * t[j] + w[1] * t[j + 1]
            cubic = cubic + w[2] * t[j + 2] + w[3] * t[j + 3]
            low, high = jnp.minimum(t[j + 1], t[j + 2]), jnp.maximum(t[j + 1], t[j + 2])
            f_col[s, lev, OFFMAX + first + j] = jnp.minimum(jnp.maximum(cubic, low), high)

    def inside(x, _):
        s, lev = x // L, lax.rem(x, L)
        for first in range(1, W - 2, ROWS):
            departures(s, lev, first, min(ROWS, W - 2 - first))
        return 0

    lax.fori_loop(0, S * L, inside, 0)
    hear(2)
    tell(3)

    edge_up.wait_recv()
    edge_down.wait_recv()
    g_down.wait_recv()
    g_up.wait_recv()

    def g_total(lev, _):
        for j in range(OFFMAX):
            g_col[lev, j] = g_col[lev, j] + g_halo[0, lev, j]
            g_col[lev, W - OFFMAX + j] = g_col[lev, W - OFFMAX + j] + g_halo[1, lev, j]
        return 0

    lax.fori_loop(0, L, g_total, 0)

    def after_mass(s, _):
        def level(lev, totals):
            totals = list(totals)
            departures(s, lev, 0, 1)
            departures(s, lev, W - 2, 2)
            for b in range(W):
                totals[b % 4] = totals[b % 4] + f_col[s, lev, OFFMAX + b] * g_col[lev, b]
            return tuple(totals)

        zero = jnp.zeros((ROWS, LANES), jnp.float32)
        totals = lax.fori_loop(0, L, level, (zero,) * 4)
        acc[S + s] = (totals[0] + totals[1]) + (totals[2] + totals[3])
        return 0

    lax.fori_loop(0, S, after_mass, 0)

    sums = jnp.sum(jnp.sum(acc[...], axis=1), axis=1, keepdims=True)
    at_row = lax.broadcasted_iota(jnp.int32, (2 * S, LANES), 0)
    at_lane = lax.broadcasted_iota(jnp.int32, (2 * S, LANES), 1)
    row_own[...] = jnp.sum(jnp.where(at_row == at_lane, sums, 0.0), axis=0, keepdims=True)

    pair = remote(row_own, row_pair, pair_send.at[0], pair_recv.at[0], partner)
    pair.start()
    pair.wait_recv()
    row_own_chip = row_own[...] + row_pair[...]
    row_side[...] = row_own_chip
    for r in range(3, rounds):
        hear(r)
        if r + 1 < rounds:
            tell(r + 1)

    way = 2 * (1 - 2 * core)
    near = [
        remote(row_side, rows_near.at[d], near_send.at[d], near_recv.at[d], away(way * (d + 1))) for d in range(reach)
    ]
    for copy in near:
        copy.start()

    def cells(s, _):
        bulk_up(s).wait_recv()
        bulk_down(s).wait_recv()

        def halo(lev, _):
            for first in (-OFFMAX, -OFFMAX + 6, W, W + 6):
                departures(s, lev, first, 6)
            return 0

        lax.fori_loop(0, L, halo, 0)

        def gather(x, _):
            lev, blk = x // blocks, lax.rem(x, blocks)
            base = blk * ROWS
            f = [f_col[s, lev, base + j] for j in range(ROWS + 2 * OFFMAX)]
            for l in range(ROWS):
                k = k_col[lev, base + l]
                bits = [(k & (1 << bit)) != 0 for bit in range(5)]
                t_in[s, lev, blk, pl.ds(l, ROWS, stride=ROWS), :] = pick(bits, f[l : l + 2 * OFFMAX + 1])
            return 0

        lax.fori_loop(0, L * blocks, gather, 0)
        return 0

    lax.fori_loop(0, S // 2, cells, 0)

    for copy in near:
        copy.wait_recv()
    sided = jnp.sum(rows_near[...], axis=0)
    last = jnp.where(core == 0, 1.0, 0.0)
    row_far_out[...] = jnp.sum(rows_near[pl.ds(0, reach - 1)], axis=0) + last * rows_near[reach - 1]
    far = remote(row_far_out, row_far, far_send.at[0], far_recv.at[0], away(way * reach))
    far.start()

    lax.fori_loop(S // 2, S - 1, cells, 0)

    far.wait_recv()
    row_pair_side = sided + row_far[...]
    row_far_out_2 = row_other.at[0]
    row_far_out_2[...] = row_pair_side
    swap = remote(row_other.at[0], row_other.at[1], pair_send.at[1], pair_recv.at[1], partner)
    swap.start()

    lax.fori_loop(S - 1, S, cells, 0)

    swap.wait_recv()
    total = row_side[...] + (row_other[0] + row_other[1])
    spread = jnp.broadcast_to(total, (S, LANES))
    at_row = lax.broadcasted_iota(jnp.int32, (S, LANES), 0)
    at_lane = lax.broadcasted_iota(jnp.int32, (S, LANES), 1)
    before = jnp.sum(jnp.where(at_lane == at_row, spread, 0.0), axis=1, keepdims=True)
    after = jnp.sum(jnp.where(at_lane == at_row + S, spread, 0.0), axis=1, keepdims=True)
    gain = jnp.zeros((S, LANES), jnp.float32)
    for s in range(S):
        gain = jnp.where(at_row == s, 1.0 + growth[s], gain)
    ratio = before * gain / after
    for s in range(S):
        factor[s] = jnp.broadcast_to(ratio[s : s + 1, :], (ROWS, LANES))

    def scale(s, _):
        def part(x, _):
            lev, blk = x // blocks, lax.rem(x, blocks)
            for l in range(ROWS):
                rows = pl.ds(l * ROWS, ROWS)
                t_in[s, lev, blk, rows, :] = t_in[s, lev, blk, rows, :] * factor[s]
            return 0

        lax.fori_loop(0, L * blocks, part, 0)
        pltpu.make_async_copy(t_in.at[s], out.at[s], out_sem.at[s]).start()
        return 0

    lax.fori_loop(0, S, scale, 0)

    edge_up.wait_send()
    edge_down.wait_send()
    g_down.wait_send()
    g_up.wait_send()
    pair.wait_send()
    swap.wait_send()
    far.wait_send()
    for copy in near:
        copy.wait_send()

    def finish(s, _):
        bulk_up(s).wait_send()
        bulk_down(s).wait_send()
        pltpu.make_async_copy(t_in.at[s], out.at[s], out_sem.at[s]).wait()
        return 0

    lax.fori_loop(0, S, finish, 0)


def to_tiles(a):
    *lead, cols, lats = a.shape
    k = len(lead)
    a = a.reshape(*lead, cols // ROWS, ROWS, lats // LANES, LANES)
    a = a.transpose(*range(k), k, k + 2, k + 1, k + 3)
    return a.reshape(*lead, cols // ROWS, lats // LANES * ROWS, LANES)


def from_tiles(a, cols, lats):
    *lead, _, _, _ = a.shape
    k = len(lead)
    a = a.reshape(*lead, cols // ROWS, lats // LANES, ROWS, LANES)
    a = a.transpose(*range(k), k, k + 2, k + 1, k + 3)
    return a.reshape(*lead, cols, lats)


def on_device(n, tracer, offsets, frac, air_before, air_after, growth):
    S, L, W, lats = tracer.shape
    tiles = to_tiles(tracer)
    f32, vmem = jnp.float32, pltpu.VMEM
    column = (ROWS, LANES)
    blocks = W // ROWS
    dma = pltpu.SemaphoreType.DMA
    reach = n // 8
    rounds = reach.bit_length()
    small = (L, blocks, ROWS * ROWS, LANES)
    result = pl.pallas_call(
        functools.partial(kernel, (S, L, W, n)),
        out_shape=jax.ShapeDtypeStruct(tiles.shape, f32),
        in_specs=[pl.BlockSpec(memory_space=pl.ANY)] * 4
        + [pl.BlockSpec(memory_space=pltpu.VMEM), pl.BlockSpec(memory_space=pltpu.SMEM)],
        out_specs=pl.BlockSpec(memory_space=pl.ANY),
        scratch_shapes=[
            vmem(tiles.shape, f32),
            vmem(small, jnp.int32),
            vmem(small, f32),
            vmem(small, f32),
            vmem((S, L, LOW + W + HIGH, *column), f32),
            vmem((L, W, *column), jnp.int32),
            vmem((L, W, *column), f32),
            vmem((L, W, *column), f32),
            vmem((L, W, *column), f32),
            vmem((2, L, OFFMAX, *column), f32),
            vmem((2, L, OFFMAX, *column), f32),
            vmem((S, L, W + 2 * OFFMAX, *column), f32),
            vmem((4, L, *column), f32),
            vmem((2 * S, *column), f32),
            vmem((S, *column), f32),
            vmem((1, LANES), f32),
            vmem((1, LANES), f32),
            vmem((reach, 1, LANES), f32),
            vmem((1, LANES), f32),
            vmem((1, LANES), f32),
            vmem((1, LANES), f32),
            vmem((2, 1, LANES), f32),
            dma((S,)),
            dma((3,)),
            dma((S,)),
            dma((2,)),
            dma((2,)),
            dma((2,)),
            dma((2,)),
            dma((2, S)),
            dma((2, S)),
            pltpu.SemaphoreType.REGULAR((rounds, 2)),
            dma((2,)),
            dma((2,)),
            dma((reach,)),
            dma((reach,)),
            dma((1,)),
            dma((1,)),
        ],
        compiler_params=pltpu.CompilerParams(collective_id=0, has_side_effects=True),
    )(tiles, to_tiles(offsets), to_tiles(air_before), to_tiles(air_after), frac, growth)
    return from_tiles(result, W, lats)


def solution(mesh):
    placed = (
        P("scen", None, "lon", None),
        P(None, "lon", None),
        P(),
        P(None, "lon", None),
        P(None, "lon", None),
        P("scen"),
    )
    return jax.shard_map(
        functools.partial(on_device, mesh.shape["lon"]),
        mesh=mesh,
        in_specs=placed,
        out_specs=P("scen", None, "lon", None),
        check_vma=False,
    )
```

time: 141 us -> 58.3 us (0.41)
  other arithmetic: 58.5 us -> 0 us
  blocking collectives: 54 us -> 0 us
  Pallas kernels: 0 us -> 53.3 us
  starting transfers between devices: 20.5 us -> 0 us
  local copies, waits for them, and re-layouts: 7.32 us -> 4.79 us
    all_to_all x1 -> x0, blocking collectives: 54 us -> none  [from_everyone(): return lax.all_to_all(copies, axis, split_axis=0, concat_axis=0, tiled=True)]
    pallas_call x0 -> x1, Pallas kernels: none -> 53.3 us  [on_device(): pl.pallas_call(functools.partial(kernel, (S, L, W, n)), out_shape=jax.Sha...]
    reduce_sum x3 -> x0, other arithmetic: 49 us -> none  [the longest x1 47.3 us: on_device(): after_local = jnp.sum(limited * air_after[None], axis=(1, 2, 3))]
    ppermute x2 -> x0, starting transfers between devices: 20.5 us -> none  [the longest x1 17.3 us: with_halo(): lax.ppermute(lax.slice_in_dim(block, 0, width, axis=dim), axis, backward)]
    mul x1 -> x0, other arithmetic: 5.11 us -> none  [on_device(): return limited * factor[:, None, None, None]]
    slice x1 -> x0, local copies, waits for them, and re-layouts: 2.98 us -> none  [with_halo(): lax.slice_in_dim(block, block.shape[dim] - width, None, axis=dim)]
    eq x1 -> x0, other arithmetic: 2.91 us -> none  [limited_values(): chosen = offsets == offset_value]
    unnamed x12 -> x1, local copies, waits for them, and re-layouts: 2.16 us -> 4.79 us
  transfers between devices with their start and end apart: 2 -> 0, of which waited for: 0 -> 0; matrix products, arithmetic and copies ran while one was open for 5% -> 0% of each run, Pallas kernels for 0% -> 0%
where the time goes in v1:
time: 58.3 us; the launch traced here: 58.1 us
  Pallas kernels  53.3 us (91%)
  local copies, waits for them, and re-layouts  4.79 us (8%)
    pallas_call x1, Pallas kernels, on_device(): pl.pallas_call(functools.partial(kernel, (S, L, W, n)), out_shape=jax.Sha...  53.3 us
    unnamed x1, local copies, waits for them, and re-layouts  4.79 us

profile of v1, /device:TPU:37, one launch (start us, length us, event | category | flops | bytes accessed | tf_op | source)
XLA Modules:
  0.0 58.1 jit_solution(18440575421046416358)
XLA Ops:
  0.0 53.3 %shard_map.64 = f32[8,4,4,64,128]{4,3,2,1,0:T(8,128)} custom-call(f32[8,4,4,64,128]{4,3,2,1,0:T(8,128)} %bitcast.26, s32[4,4,64,128]{3,2,1,0:T(8,128)} %bitcast.27, f32[4,4,64,128]{3,2,1,0:T(8,128)} %bitcast.28, f32[4,4,64,128]{3,2,1,0:T(8,128)} %bitcast.29, f32[4,1024]{1,0:T(4,128)} %frac.1, f32[8]{0:T(128)} %growth.1), custom_call_target="tpu_custom_call" | custom-call | tf_op jit(solution)/shard_map/pallas_call | solution.py:424
  53.3 4.8 %copy.8 = f32[8,4,32,1024]{3,2,1,0:T(8,128)} copy(f32[8,4,32,1024]{3,2,1,0:T(8,128)} %bitcast.25) | data formatting | bytes 8388608

commit v2 on v1

--- a/solution.py
+++ b/solution.py
@@ -42,6 +42,8 @@
     growth,
     out,
     t_in,
+    frac_in,
+    growth_in,
     off_in,
     ab_in,
     aa_in,
@@ -58,14 +60,13 @@
     factor,
     row_own,
     row_pair,
+    row_chip,
     rows_near,
     row_far_out,
-    row_far,
-    row_side,
-    row_other,
+    rows_far,
+    edge_in_sem,
     in_sem,
     small_in_sem,
-    out_sem,
     edge_send,
     edge_recv,
     g_send,
@@ -95,14 +96,24 @@
     for to in (left, right):
         pl.semaphore_signal(barrier, inc=1, device_id={"lon": to}, device_id_type=MESH)
 
+    load_edges = [
+        pltpu.make_async_copy(tracer.at[:, :, blk], t_in.at[:, :, blk], edge_in_sem.at[i])
+        for i, blk in enumerate((0, blocks - 1))
+    ]
     load_off = pltpu.make_async_copy(offsets, off_in, small_in_sem.at[0])
     load_aa = pltpu.make_async_copy(air_after, aa_in, small_in_sem.at[1])
     load_ab = pltpu.make_async_copy(air_before, ab_in, small_in_sem.at[2])
-    load_off.start()
-    load_aa.start()
-    load_ab.start()
+    load_frac = pltpu.make_async_copy(frac, frac_in, small_in_sem.at[3])
+    load_growth = pltpu.make_async_copy(growth, growth_in, small_in_sem.at[4])
+
+    def load_inner(s):
+        inner = pl.ds(1, blocks - 2)
+        return pltpu.make_async_copy(tracer.at[s, :, inner], t_in.at[s, :, inner], in_sem.at[s])
+
+    for copy in (*load_edges, load_off, load_aa, load_frac, load_ab, load_growth):
+        copy.start()
     for s in range(S):
-        pltpu.make_async_copy(tracer.at[s], t_in.at[s], in_sem.at[s]).start()
+        load_inner(s).start()
 
     def remote(src, dst, send, recv, to):
         return pltpu.make_async_remote_copy(
@@ -134,10 +145,12 @@
 
     rounds = know.shape[0]
 
+    steps = [2**r for r in range(rounds - 1)] + [1]
+
     def tell(r):
         if r >= rounds:
             return
-        for side, distance in ((0, 2**r), (1, -(2**r))):
+        for side, distance in ((0, steps[r]), (1, -steps[r])):
             pl.semaphore_signal(know.at[r, side], inc=1, device_id={"lon": away(distance)}, device_id_type=MESH)
 
     def hear(r):
@@ -146,8 +159,22 @@
         for side in range(2):
             pl.semaphore_wait(know.at[r, side], 1)
 
+    for copy in load_edges:
+        copy.wait()
+
+    def relay_edges(s, _):
+        for lev in range(L):
+            for blk, l in ((0, 0), (0, 1), (blocks - 1, ROWS - 1)):
+                t_col[s, lev, LOW + blk * ROWS + l] = t_in[s, lev, blk, pl.ds(l, ROWS, stride=ROWS), :]
+        return 0
+
+    lax.fori_loop(0, S, relay_edges, 0)
     load_off.wait()
     load_aa.wait()
+    pl.semaphore_wait(barrier, 2)
+    edge_down.start()
+    edge_up.start()
+    tell(0)
 
     def relay_small(x, _):
         lev, blk = x // blocks, lax.rem(x, blocks)
@@ -172,17 +199,16 @@
         return 0
 
     lax.fori_loop(0, L, g_sides, 0)
-
+    load_frac.wait()
     for lev in range(L):
         for j in range(ROWS):
-            weight[0, lev, j : j + 1, :] = frac[lev : lev + 1, j * LANES : (j + 1) * LANES]
+            weight[0, lev, j : j + 1, :] = frac_in[lev : lev + 1, j * LANES : (j + 1) * LANES]
         for tap, w in enumerate(cubic_weights(weight[0, lev])):
             weight[tap, lev] = w
-
-    pl.semaphore_wait(barrier, 2)
     g_down.start()
     g_up.start()
-    tell(0)
+    hear(0)
+    tell(1)
 
     load_ab.wait()
 
@@ -194,28 +220,30 @@
 
     lax.fori_loop(0, L * blocks, relay_before, 0)
 
+    zero = jnp.zeros((ROWS, LANES), jnp.float32)
+
     def relay_species(s, _):
-        pltpu.make_async_copy(tracer.at[s], t_in.at[s], in_sem.at[s]).wait()
-
-        def relay(x, totals):
-            lev, blk = x // blocks, lax.rem(x, blocks)
+        load_inner(s).wait()
+
+        def relay(lev, totals):
             totals = list(totals)
-            for l in range(ROWS):
-                value = t_in[s, lev, blk, pl.ds(l, ROWS, stride=ROWS), :]
-                t_col[s, lev, LOW + blk * ROWS + l] = value
-                totals[l % 4] = totals[l % 4] + value * ab_col[lev, blk * ROWS + l]
+            for i in range(W):
+                blk, l = divmod(i, ROWS)
+                if 2 <= i < W - 1:
+                    value = t_in[s, lev, blk, pl.ds(l, ROWS, stride=ROWS), :]
+                    t_col[s, lev, LOW + i] = value
+                else:
+                    value = t_col[s, lev, LOW + i]
+                totals[i % 4] = totals[i % 4] + value * ab_col[lev, i]
             return tuple(totals)
 
-        zero = jnp.zeros((ROWS, LANES), jnp.float32)
-        totals = lax.fori_loop(0, L * blocks, relay, (zero,) * 4)
+        totals = lax.fori_loop(0, L, relay, (zero,) * 4)
         acc[s] = (totals[0] + totals[1]) + (totals[2] + totals[3])
         return 0
 
     lax.fori_loop(0, S, relay_species, 0)
-    hear(0)
-    tell(1)
-    edge_up.start()
-    edge_down.start()
+    hear(1)
+    tell(2)
 
     def send_bulk(s, _):
         bulk_up(s).start()
@@ -230,56 +258,65 @@
         return 0
 
     lax.fori_loop(0, L, g_inside, 0)
-    hear(1)
-    tell(2)
+    hear(2)
+    tell(3)
 
     def departures(s, lev, first, count):
         w = [weight[tap, lev] for tap in range(4)]
         t = [t_col[s, lev, LOW + first - 1 + j] for j in range(count + 3)]
+        values = []
         for j in range(count):
             cubic = w[0] * t[j] + w[1] * t[j + 1]
             cubic = cubic + w[2] * t[j + 2] + w[3] * t[j + 3]
             low, high = jnp.minimum(t[j + 1], t[j + 2]), jnp.maximum(t[j + 1], t[j + 2])
-            f_col[s, lev, OFFMAX + first + j] = jnp.minimum(jnp.maximum(cubic, low), high)
-
-    def inside(x, _):
-        s, lev = x // L, lax.rem(x, L)
-        for first in range(1, W - 2, ROWS):
-            departures(s, lev, first, min(ROWS, W - 2 - first))
-        return 0
-
-    lax.fori_loop(0, S * L, inside, 0)
-    hear(2)
-    tell(3)
+            values.append(jnp.minimum(jnp.maximum(cubic, low), high))
+            f_col[s, lev, OFFMAX + first + j] = values[-1]
+        return values
+
+    def inside(s, _):
+        def level(lev, totals):
+            totals = list(totals)
+            for first in range(1, W - 2, ROWS):
+                for j, value in enumerate(departures(s, lev, first, min(ROWS, W - 2 - first))):
+                    totals[j % 4] = totals[j % 4] + value * g_col[lev, first + j]
+            return tuple(totals)
+
+        totals = lax.fori_loop(0, L, level, (zero,) * 4)
+        acc[S + s] = (totals[0] + totals[1]) + (totals[2] + totals[3])
+        return 0
+
+    lax.fori_loop(0, S, inside, 0)
+    hear(3)
+    tell(4)
 
     edge_up.wait_recv()
     edge_down.wait_recv()
     g_down.wait_recv()
     g_up.wait_recv()
 
-    def g_total(lev, _):
-        for j in range(OFFMAX):
-            g_col[lev, j] = g_col[lev, j] + g_halo[0, lev, j]
-            g_col[lev, W - OFFMAX + j] = g_col[lev, W - OFFMAX + j] + g_halo[1, lev, j]
-        return 0
-
-    lax.fori_loop(0, L, g_total, 0)
-
-    def after_mass(s, _):
-        def level(lev, totals):
-            totals = list(totals)
-            departures(s, lev, 0, 1)
-            departures(s, lev, W - 2, 2)
-            for b in range(W):
-                totals[b % 4] = totals[b % 4] + f_col[s, lev, OFFMAX + b] * g_col[lev, b]
-            return tuple(totals)
-
-        zero = jnp.zeros((ROWS, LANES), jnp.float32)
-        totals = lax.fori_loop(0, L, level, (zero,) * 4)
-        acc[S + s] = (totals[0] + totals[1]) + (totals[2] + totals[3])
-        return 0
-
-    lax.fori_loop(0, S, after_mass, 0)
+    def outer_mass(lev, totals):
+        g_low = [g_halo[0, lev, j] for j in range(OFFMAX)]
+        g_high = [g_halo[1, lev, j] for j in range(OFFMAX)]
+        sums = []
+        for s in range(S):
+            parts = [totals[s], zero]
+            (first,) = departures(s, lev, 0, 1)
+            last = departures(s, lev, W - 2, 2)
+            parts[0] = parts[0] + first * g_col[lev, 0]
+            parts[1] = parts[1] + last[0] * g_col[lev, W - 2]
+            parts[1] = parts[1] + last[1] * g_col[lev, W - 1]
+            for j in range(OFFMAX):
+                low = first if j == 0 else f_col[s, lev, OFFMAX + j]
+                at = W - OFFMAX + j
+                high = last[at - W + 2] if at >= W - 2 else f_col[s, lev, OFFMAX + at]
+                parts[0] = parts[0] + low * g_low[j]
+                parts[1] = parts[1] + high * g_high[j]
+            sums.append(parts[0] + parts[1])
+        return tuple(sums)
+
+    totals = lax.fori_loop(0, L, outer_mass, tuple(acc[S + s] for s in range(S)))
+    for s in range(S):
+        acc[S + s] = totals[s]
 
     sums = jnp.sum(jnp.sum(acc[...], axis=1), axis=1, keepdims=True)
     at_row = lax.broadcasted_iota(jnp.int32, (2 * S, LANES), 0)
@@ -289,19 +326,26 @@
     pair = remote(row_own, row_pair, pair_send.at[0], pair_recv.at[0], partner)
     pair.start()
     pair.wait_recv()
-    row_own_chip = row_own[...] + row_pair[...]
-    row_side[...] = row_own_chip
-    for r in range(3, rounds):
+    row_chip[...] = row_own[...] + row_pair[...]
+    for r in range(4, rounds):
         hear(r)
-        if r + 1 < rounds:
-            tell(r + 1)
+        tell(r + 1)
 
     way = 2 * (1 - 2 * core)
+
+    def to_chip(d, at):
+        return away(way * d - core + at)
+
     near = [
-        remote(row_side, rows_near.at[d], near_send.at[d], near_recv.at[d], away(way * (d + 1))) for d in range(reach)
+        remote(row_chip, rows_near.at[core, d], near_send.at[at, d], near_recv.at[core, d], to_chip(d + 1, at))
+        for d in range(reach)
+        for at in range(2)
     ]
     for copy in near:
         copy.start()
+
+    def near_from(side, d):
+        return remote(row_chip, rows_near.at[side, d], near_send.at[0, d], near_recv.at[side, d], partner)
 
     def cells(s, _):
         bulk_up(s).wait_recv()
@@ -321,35 +365,33 @@
             for l in range(ROWS):
                 k = k_col[lev, base + l]
                 bits = [(k & (1 << bit)) != 0 for bit in range(5)]
-                t_in[s, lev, blk, pl.ds(l, ROWS, stride=ROWS), :] = pick(bits, f[l : l + 2 * OFFMAX + 1])
+                out[s, lev, blk, pl.ds(l, ROWS, stride=ROWS), :] = pick(bits, f[l : l + 2 * OFFMAX + 1])
             return 0
 
         lax.fori_loop(0, L * blocks, gather, 0)
         return 0
 
-    lax.fori_loop(0, S // 2, cells, 0)
-
-    for copy in near:
-        copy.wait_recv()
-    sided = jnp.sum(rows_near[...], axis=0)
-    last = jnp.where(core == 0, 1.0, 0.0)
-    row_far_out[...] = jnp.sum(rows_near[pl.ds(0, reach - 1)], axis=0) + last * rows_near[reach - 1]
-    far = remote(row_far_out, row_far, far_send.at[0], far_recv.at[0], away(way * reach))
-    far.start()
-
-    lax.fori_loop(S // 2, S - 1, cells, 0)
-
-    far.wait_recv()
-    row_pair_side = sided + row_far[...]
-    row_far_out_2 = row_other.at[0]
-    row_far_out_2[...] = row_pair_side
-    swap = remote(row_other.at[0], row_other.at[1], pair_send.at[1], pair_recv.at[1], partner)
-    swap.start()
-
-    lax.fori_loop(S - 1, S, cells, 0)
-
-    swap.wait_recv()
-    total = row_side[...] + (row_other[0] + row_other[1])
+    early = S // 2 - 1
+    lax.fori_loop(0, early, cells, 0)
+
+    for side in range(2):
+        for d in range(reach):
+            near_from(side, d).wait_recv()
+    mine = jnp.sum(rows_near[core, pl.ds(0, reach - 1)], axis=0)
+    row_far_out[...] = mine + jnp.where(core == 0, 1.0, 0.0) * rows_near[core, reach - 1]
+    far = [
+        remote(row_far_out, rows_far.at[core], far_send.at[at], far_recv.at[core], to_chip(reach, at)) for at in range(2)
+    ]
+    for copy in far:
+        copy.start()
+    near_total = row_chip[...] + jnp.sum(rows_near[0], axis=0) + jnp.sum(rows_near[1], axis=0)
+
+    lax.fori_loop(early, S, cells, 0)
+
+    for side in range(2):
+        remote(row_far_out, rows_far.at[side], far_send.at[0], far_recv.at[side], partner).wait_recv()
+    load_growth.wait()
+    total = near_total + (rows_far[0] + rows_far[1])
     spread = jnp.broadcast_to(total, (S, LANES))
     at_row = lax.broadcasted_iota(jnp.int32, (S, LANES), 0)
     at_lane = lax.broadcasted_iota(jnp.int32, (S, LANES), 1)
@@ -357,7 +399,7 @@
     after = jnp.sum(jnp.where(at_lane == at_row + S, spread, 0.0), axis=1, keepdims=True)
     gain = jnp.zeros((S, LANES), jnp.float32)
     for s in range(S):
-        gain = jnp.where(at_row == s, 1.0 + growth[s], gain)
+        gain = jnp.where(at_row == s, 1.0 + growth_in[s], gain)
     ratio = before * gain / after
     for s in range(S):
         factor[s] = jnp.broadcast_to(ratio[s : s + 1, :], (ROWS, LANES))
@@ -367,11 +409,10 @@
             lev, blk = x // blocks, lax.rem(x, blocks)
             for l in range(ROWS):
                 rows = pl.ds(l * ROWS, ROWS)
-                t_in[s, lev, blk, rows, :] = t_in[s, lev, blk, rows, :] * factor[s]
+                out[s, lev, blk, rows, :] = out[s, lev, blk, rows, :] * factor[s]
             return 0
 
         lax.fori_loop(0, L * blocks, part, 0)
-        pltpu.make_async_copy(t_in.at[s], out.at[s], out_sem.at[s]).start()
         return 0
 
     lax.fori_loop(0, S, scale, 0)
@@ -381,15 +422,12 @@
     g_down.wait_send()
     g_up.wait_send()
     pair.wait_send()
-    swap.wait_send()
-    far.wait_send()
-    for copy in near:
+    for copy in (*near, *far):
         copy.wait_send()
 
     def finish(s, _):
         bulk_up(s).wait_send()
         bulk_down(s).wait_send()
-        pltpu.make_async_copy(t_in.at[s], out.at[s], out_sem.at[s]).wait()
         return 0
 
     lax.fori_loop(0, S, finish, 0)
@@ -409,6 +447,10 @@
     a = a.reshape(*lead, cols // ROWS, lats // LANES, ROWS, LANES)
     a = a.transpose(*range(k), k, k + 2, k + 1, k + 3)
     return a.reshape(*lead, cols, lats)
+
+
+def in_hbm(a):
+    return pltpu.with_memory_space_constraint(a, pltpu.HBM)
 
 
 def on_device(n, tracer, offsets, frac, air_before, air_after, growth):
@@ -419,16 +461,18 @@
     blocks = W // ROWS
     dma = pltpu.SemaphoreType.DMA
     reach = n // 8
-    rounds = reach.bit_length()
+    rounds = reach.bit_length() + 1
     small = (L, blocks, ROWS * ROWS, LANES)
     result = pl.pallas_call(
         functools.partial(kernel, (S, L, W, n)),
-        out_shape=jax.ShapeDtypeStruct(tiles.shape, f32),
-        in_specs=[pl.BlockSpec(memory_space=pl.ANY)] * 4
-        + [pl.BlockSpec(memory_space=pltpu.VMEM), pl.BlockSpec(memory_space=pltpu.SMEM)],
-        out_specs=pl.BlockSpec(memory_space=pl.ANY),
+        out_shape=pltpu.VMEM(tiles.shape, f32),
+        in_specs=[pl.BlockSpec(memory_space=pltpu.HBM)] * 6,
+
+        out_specs=pl.BlockSpec(memory_space=pltpu.VMEM),
         scratch_shapes=[
             vmem(tiles.shape, f32),
+            vmem(frac.shape, f32),
+            pltpu.SMEM(growth.shape, f32),
             vmem(small, jnp.int32),
             vmem(small, f32),
             vmem(small, f32),
@@ -445,14 +489,13 @@
             vmem((S, *column), f32),
             vmem((1, LANES), f32),
             vmem((1, LANES), f32),
-            vmem((reach, 1, LANES), f32),
             vmem((1, LANES), f32),
-            vmem((1, LANES), f32),
+            vmem((2, reach, 1, LANES), f32),
             vmem((1, LANES), f32),
             vmem((2, 1, LANES), f32),
+            dma((2,)),
             dma((S,)),
-            dma((3,)),
-            dma((S,)),
+            dma((5,)),
             dma((2,)),
             dma((2,)),
             dma((2,)),
@@ -460,15 +503,15 @@
             dma((2, S)),
             dma((2, S)),
             pltpu.SemaphoreType.REGULAR((rounds, 2)),
-            dma((2,)),
-            dma((2,)),
-            dma((reach,)),
-            dma((reach,)),
             dma((1,)),
             dma((1,)),
+            dma((2, reach)),
+            dma((2, reach)),
+            dma((2,)),
+            dma((2,)),
         ],
-        compiler_params=pltpu.CompilerParams(collective_id=0, has_side_effects=True),
-    )(tiles, to_tiles(offsets), to_tiles(air_before), to_tiles(air_after), frac, growth)
+        compiler_params=pltpu.CompilerParams(collective_id=0, has_side_effects=True, vmem_limit_bytes=44 * 2**20),
+    )(*map(in_hbm, (tiles, to_tiles(offsets), to_tiles(air_before), to_tiles(air_after), frac, growth)))
     return from_tiles(result, W, lats)
 
 

time: 58.3 us -> 52.6 us (0.902)
  Pallas kernels: 53.3 us -> 50.3 us
  local copies, waits for them, and re-layouts: 4.79 us -> 2.02 us
    pallas_call x1, Pallas kernels: 53.3 us -> 50.3 us  [on_device(): pl.pallas_call(functools.partial(kernel, (S, L, W, n)), out_shape=pltpu.V...]
    unnamed x1, local copies, waits for them, and re-layouts: 4.79 us -> 2.02 us
where the time goes in v2:
time: 52.6 us; the launch traced here: 52.3 us
  Pallas kernels  50.3 us (96%)
  local copies, waits for them, and re-layouts  2.02 us (4%)
    pallas_call x1, Pallas kernels, on_device(): pl.pallas_call(functools.partial(kernel, (S, L, W, n)), out_shape=pltpu.V...  50.3 us
    unnamed x1, local copies, waits for them, and re-layouts  2.02 us

profile of v2, /device:TPU:37, one launch (start us, length us, event | category | flops | bytes accessed | tf_op | source)
XLA Modules:
  0.0 52.3 jit_solution(14145117501842861337)
XLA Ops:
  0.0 50.3 %shard_map.64 = f32[8,4,4,64,128]{4,3,2,1,0:T(8,128)S(1)} custom-call(f32[8,4,4,64,128]{4,3,2,1,0:T(8,128)} %bitcast.26, s32[4,4,64,128]{3,2,1,0:T(8,128)} %bitcast.27, f32[4,4,64,128]{3,2,1,0:T(8,128)} %bitcast.28, f32[4,4,64,128]{3,2,1,0:T(8,128)} %bitcast.29, f32[4,1024]{1,0:T(4,128)} %frac.1, f32[8]{0:T(128)} %growth.1), custom_call_target="tpu_custom_call" | custom-call | tf_op jit(solution)/shard_map/pallas_call | solution.py:466
  50.3 2.0 %copy.8 = f32[8,4,32,1024]{3,2,1,0:T(8,128)} copy(f32[8,4,32,1024]{3,2,1,0:T(8,128)S(1)} %bitcast.25) | data formatting | bytes 8388608

commit v3 on v2

--- a/solution.py
+++ b/solution.py
@@ -12,7 +12,16 @@
 ROWS = 8
 LOW = OFFMAX + 1
 HIGH = OFFMAX + 2
+NEAR = 5
 MESH = pl.DeviceIdType.MESH
+
+
+def know_steps(known, wanted):
+    steps = []
+    while known < wanted:
+        steps.append(min(known, wanted - known))
+        known += steps[-1]
+    return steps
 
 
 def cubic_weights(fraction):
@@ -41,6 +50,7 @@
     frac,
     growth,
     out,
+    factor,
     t_in,
     frac_in,
     growth_in,
@@ -57,7 +67,6 @@
     f_col,
     weight,
     acc,
-    factor,
     row_own,
     row_pair,
     row_chip,
@@ -93,8 +102,10 @@
         return lax.rem(me + distance + n, n)
 
     barrier = pltpu.get_barrier_semaphore()
-    for to in (left, right):
-        pl.semaphore_signal(barrier, inc=1, device_id={"lon": to}, device_id_type=MESH)
+    close_by = min(NEAR, n // 2 - 1)
+    for distance in range(1, close_by + 1):
+        for to in (away(distance), away(-distance)):
+            pl.semaphore_signal(barrier, inc=1, device_id={"lon": to}, device_id_type=MESH)
 
     load_edges = [
         pltpu.make_async_copy(tracer.at[:, :, blk], t_in.at[:, :, blk], edge_in_sem.at[i])
@@ -143,9 +154,8 @@
             left,
         )
 
-    rounds = know.shape[0]
-
-    steps = [2**r for r in range(rounds - 1)] + [1]
+    steps = know_steps(close_by, 2 * reach + 1)
+    rounds = len(steps)
 
     def tell(r):
         if r >= rounds:
@@ -171,7 +181,7 @@
     lax.fori_loop(0, S, relay_edges, 0)
     load_off.wait()
     load_aa.wait()
-    pl.semaphore_wait(barrier, 2)
+    pl.semaphore_wait(barrier, 2 * close_by)
     edge_down.start()
     edge_up.start()
     tell(0)
@@ -207,9 +217,6 @@
             weight[tap, lev] = w
     g_down.start()
     g_up.start()
-    hear(0)
-    tell(1)
-
     load_ab.wait()
 
     def relay_before(x, _):
@@ -242,9 +249,6 @@
         return 0
 
     lax.fori_loop(0, S, relay_species, 0)
-    hear(1)
-    tell(2)
-
     def send_bulk(s, _):
         bulk_up(s).start()
         bulk_down(s).start()
@@ -257,9 +261,10 @@
             g_col[lev, b] = weight_of(lev, b)
         return 0
 
-    lax.fori_loop(0, L, g_inside, 0)
-    hear(2)
-    tell(3)
+    lax.fori_loop(0, L // 2, g_inside, 0)
+    hear(0)
+    tell(1)
+    lax.fori_loop(L // 2, L, g_inside, 0)
 
     def departures(s, lev, first, count):
         w = [weight[tap, lev] for tap in range(4)]
@@ -286,8 +291,6 @@
         return 0
 
     lax.fori_loop(0, S, inside, 0)
-    hear(3)
-    tell(4)
 
     edge_up.wait_recv()
     edge_down.wait_recv()
@@ -327,7 +330,7 @@
     pair.start()
     pair.wait_recv()
     row_chip[...] = row_own[...] + row_pair[...]
-    for r in range(4, rounds):
+    for r in range(1, rounds):
         hear(r)
         tell(r + 1)
 
@@ -404,19 +407,6 @@
     for s in range(S):
         factor[s] = jnp.broadcast_to(ratio[s : s + 1, :], (ROWS, LANES))
 
-    def scale(s, _):
-        def part(x, _):
-            lev, blk = x // blocks, lax.rem(x, blocks)
-            for l in range(ROWS):
-                rows = pl.ds(l * ROWS, ROWS)
-                out[s, lev, blk, rows, :] = out[s, lev, blk, rows, :] * factor[s]
-            return 0
-
-        lax.fori_loop(0, L * blocks, part, 0)
-        return 0
-
-    lax.fori_loop(0, S, scale, 0)
-
     edge_up.wait_send()
     edge_down.wait_send()
     g_down.wait_send()
@@ -431,6 +421,30 @@
         return 0
 
     lax.fori_loop(0, S, finish, 0)
+
+
+def scale_kernel(limited, factor, out, scaled, sem):
+    S, L = limited.shape[:2]
+
+    def put(s):
+        return pltpu.make_async_copy(scaled.at[s], out.at[s], sem.at[s])
+
+    def scale(s, _):
+        gain = factor[s]
+
+        def level(lev, _):
+            for blk in range(limited.shape[2]):
+                for row in range(0, limited.shape[3], ROWS):
+                    scaled[s, lev, blk, pl.ds(row, ROWS), :] = limited[s, lev, blk, pl.ds(row, ROWS), :] * gain
+            return 0
+
+        lax.fori_loop(0, L, level, 0)
+        put(s).start()
+        return 0
+
+    lax.fori_loop(0, S, scale, 0)
+    for s in range(S):
+        put(s).wait()
 
 
 def to_tiles(a):
@@ -461,14 +475,14 @@
     blocks = W // ROWS
     dma = pltpu.SemaphoreType.DMA
     reach = n // 8
-    rounds = reach.bit_length() + 1
+    rounds = len(know_steps(min(NEAR, n // 2 - 1), 2 * reach + 1))
     small = (L, blocks, ROWS * ROWS, LANES)
-    result = pl.pallas_call(
+    limited, factor = pl.pallas_call(
         functools.partial(kernel, (S, L, W, n)),
-        out_shape=pltpu.VMEM(tiles.shape, f32),
+        out_shape=[pltpu.VMEM(tiles.shape, f32), pltpu.VMEM((S, *column), f32)],
         in_specs=[pl.BlockSpec(memory_space=pltpu.HBM)] * 6,
 
-        out_specs=pl.BlockSpec(memory_space=pltpu.VMEM),
+        out_specs=[pl.BlockSpec(memory_space=pltpu.VMEM)] * 2,
         scratch_shapes=[
             vmem(tiles.shape, f32),
             vmem(frac.shape, f32),
@@ -486,7 +500,6 @@
             vmem((S, L, W + 2 * OFFMAX, *column), f32),
             vmem((4, L, *column), f32),
             vmem((2 * S, *column), f32),
-            vmem((S, *column), f32),
             vmem((1, LANES), f32),
             vmem((1, LANES), f32),
             vmem((1, LANES), f32),
@@ -512,6 +525,14 @@
         ],
         compiler_params=pltpu.CompilerParams(collective_id=0, has_side_effects=True, vmem_limit_bytes=44 * 2**20),
     )(*map(in_hbm, (tiles, to_tiles(offsets), to_tiles(air_before), to_tiles(air_after), frac, growth)))
+    result = pl.pallas_call(
+        scale_kernel,
+        out_shape=jax.ShapeDtypeStruct(tiles.shape, f32),
+        in_specs=[pl.BlockSpec(memory_space=pltpu.VMEM)] * 2,
+        out_specs=pl.BlockSpec(memory_space=pl.ANY),
+        scratch_shapes=[vmem(tiles.shape, f32), dma((S,))],
+        compiler_params=pltpu.CompilerParams(vmem_limit_bytes=24 * 2**20),
+    )(limited, factor)
     return from_tiles(result, W, lats)
 
 

time: 52.6 us -> 53.2 us (1.011)
  Pallas kernels: 50.3 us -> 53.1 us
  local copies, waits for them, and re-layouts: 2.02 us -> 0 us
    pallas_call x1 -> x2, Pallas kernels: 50.3 us -> 53.1 us  [the longest x1 51 us: on_device(): pl.pallas_call(functools.partial(kernel, (S, L, W, n)), out_shape=[pltpu....]
    unnamed x1 -> x0, local copies, waits for them, and re-layouts: 2.02 us -> none
where the time goes in v3:
time: 53.2 us; the launch traced here: 53.1 us
  Pallas kernels  53.1 us (100%)
    pallas_call x1, Pallas kernels, on_device(): pl.pallas_call(functools.partial(kernel, (S, L, W, n)), out_shape=[pltpu....  51 us
    pallas_call x1, Pallas kernels, on_device(): pl.pallas_call(scale_kernel, out_shape=jax.ShapeDtypeStruct(tiles.shape,...  2.12 us

profile of v3, /device:TPU:37, one launch (start us, length us, event | category | flops | bytes accessed | tf_op | source)
XLA Modules:
  0.0 53.1 jit_solution(13824526937170613095)
XLA Ops:
  0.0 51.0 %shard_map.64 = (f32[8,4,4,64,128]{4,3,2,1,0:T(8,128)S(1)}, f32[8,8,128]{2,1,0:T(8,128)S(1)}) custom-call(f32[8,4,4,64,128]{4,3,2,1,0:T(8,128)} %bitcast.25, s32[4,4,64,128]{3,2,1,0:T(8,128)} %bitcast.26, f32[4,4,64,128]{3,2,1,0:T(8,128)} %bitcast.27, f32[4,4,64,128]{3,2,1,0:T(8,128)} %bitcast.28, f32[4,1024]{1,0:T(4,128)} %frac.1, f32[8]{0:T(128)} %growth.1), custom_call_target="tpu_custom_call" | custom-call | tf_op jit(solution)/shard_map/pallas_call | solution.py:480
  51.0 2.1 %shard_map.65 = f32[8,4,4,64,128]{4,3,2,1,0:T(8,128)} custom-call(f32[8,4,4,64,128]{4,3,2,1,0:T(8,128)S(1)} %get-tuple-element.7.limited, f32[8,8,128]{2,1,0:T(8,128)S(1)} %get-tuple-element.8.factor), custom_call_target="tpu_custom_call" | custom-call | tf_op jit(solution)/shard_map/pallas_call | solution.py:528

commit v4 on v3

--- a/solution.py
+++ b/solution.py
@@ -12,7 +12,6 @@
 ROWS = 8
 LOW = OFFMAX + 1
 HIGH = OFFMAX + 2
-NEAR = 5
 MESH = pl.DeviceIdType.MESH
 
 
@@ -52,6 +51,7 @@
     out,
     factor,
     t_in,
+    t_halo,
     frac_in,
     growth_in,
     off_in,
@@ -76,6 +76,8 @@
     edge_in_sem,
     in_sem,
     small_in_sem,
+    tile_send,
+    tile_recv,
     edge_send,
     edge_recv,
     g_send,
@@ -102,10 +104,8 @@
         return lax.rem(me + distance + n, n)
 
     barrier = pltpu.get_barrier_semaphore()
-    close_by = min(NEAR, n // 2 - 1)
-    for distance in range(1, close_by + 1):
-        for to in (away(distance), away(-distance)):
-            pl.semaphore_signal(barrier, inc=1, device_id={"lon": to}, device_id_type=MESH)
+    for to in (left, right):
+        pl.semaphore_signal(barrier, inc=1, device_id={"lon": to}, device_id_type=MESH)
 
     load_edges = [
         pltpu.make_async_copy(tracer.at[:, :, blk], t_in.at[:, :, blk], edge_in_sem.at[i])
@@ -131,30 +131,47 @@
             src_ref=src, dst_ref=dst, send_sem=send, recv_sem=recv, device_id={"lon": to}, device_id_type=MESH
         )
 
+    tile_up = remote(tracer.at[0, :, blocks - 1], t_halo.at[0], tile_send.at[0], tile_recv.at[0], right)
+    tile_down = remote(tracer.at[0, :, 0], t_halo.at[1], tile_send.at[1], tile_recv.at[1], left)
+    others = pl.ds(1, S - 1)
     edge_up = remote(
-        t_col.at[:, :, pl.ds(LOW + W - 1, 1)], t_col.at[:, :, pl.ds(LOW - 1, 1)], edge_send.at[0], edge_recv.at[0], right
+        t_col.at[others, :, pl.ds(LOW + W - 1, 1)], t_col.at[others, :, pl.ds(LOW - 1, 1)], edge_send.at[0], edge_recv.at[0], right
     )
     edge_down = remote(
-        t_col.at[:, :, pl.ds(LOW, 2)], t_col.at[:, :, pl.ds(LOW + W, 2)], edge_send.at[1], edge_recv.at[1], left
+        t_col.at[others, :, pl.ds(LOW, 2)], t_col.at[others, :, pl.ds(LOW + W, 2)], edge_send.at[1], edge_recv.at[1], left
     )
     g_down = remote(g_out.at[0], g_halo.at[1], g_send.at[0], g_recv.at[0], left)
     g_up = remote(g_out.at[1], g_halo.at[0], g_send.at[1], g_recv.at[1], right)
 
-    def bulk_up(s):
-        return remote(
-            t_col.at[s, :, pl.ds(W, OFFMAX)], t_col.at[s, :, pl.ds(0, OFFMAX)], bulk_send.at[0, s], bulk_recv.at[0, s], right
+    def bulk(s, sem, levels, up_count, down_first):
+        down_count = HIGH - down_first
+        return (
+            remote(
+                t_col.at[s, levels, pl.ds(W, up_count)],
+                t_col.at[s, levels, pl.ds(0, up_count)],
+                bulk_send.at[0, sem],
+                bulk_recv.at[0, sem],
+                right,
+            ),
+            remote(
+                t_col.at[s, levels, pl.ds(LOW + down_first, down_count)],
+                t_col.at[s, levels, pl.ds(LOW + W + down_first, down_count)],
+                bulk_send.at[1, sem],
+                bulk_recv.at[1, sem],
+                left,
+            ),
         )
 
-    def bulk_down(s):
-        return remote(
-            t_col.at[s, :, pl.ds(LOW + 2, OFFMAX)],
-            t_col.at[s, :, pl.ds(LOW + W + 2, OFFMAX)],
-            bulk_send.at[1, s],
-            bulk_recv.at[1, s],
-            left,
-        )
-
-    steps = know_steps(close_by, 2 * reach + 1)
+    def bulk_first():
+        return bulk(0, 0, pl.ds(0, L), LOW - ROWS, ROWS)
+
+    def bulk_inner(s):
+        return bulk(s, s, pl.ds(0, L), LOW - 1, 2)
+
+    def bulk_last(lev):
+        return bulk(S - 1, S - 1 + lev, pl.ds(lev, 1), LOW - 1, 2)
+
+    steps = know_steps(1, 2 * reach + 1)
     rounds = len(steps)
 
     def tell(r):
@@ -169,6 +186,11 @@
         for side in range(2):
             pl.semaphore_wait(know.at[r, side], 1)
 
+    pl.semaphore_wait(barrier, 2)
+    tile_up.start()
+    tile_down.start()
+    tell(0)
+
     for copy in load_edges:
         copy.wait()
 
@@ -179,12 +201,10 @@
         return 0
 
     lax.fori_loop(0, S, relay_edges, 0)
+    edge_down.start()
+    edge_up.start()
     load_off.wait()
     load_aa.wait()
-    pl.semaphore_wait(barrier, 2 * close_by)
-    edge_down.start()
-    edge_up.start()
-    tell(0)
 
     def relay_small(x, _):
         lev, blk = x // blocks, lax.rem(x, blocks)
@@ -217,6 +237,8 @@
             weight[tap, lev] = w
     g_down.start()
     g_up.start()
+    hear(0)
+    tell(1)
     load_ab.wait()
 
     def relay_before(x, _):
@@ -249,22 +271,27 @@
         return 0
 
     lax.fori_loop(0, S, relay_species, 0)
+    for copy in bulk_first():
+        copy.start()
+
     def send_bulk(s, _):
-        bulk_up(s).start()
-        bulk_down(s).start()
-        return 0
-
-    lax.fori_loop(0, S, send_bulk, 0)
+        for copy in bulk_inner(s):
+            copy.start()
+        return 0
+
+    lax.fori_loop(1, S - 1, send_bulk, 0)
+    for lev in range(L):
+        for copy in bulk_last(lev):
+            copy.start()
+    hear(1)
+    tell(2)
 
     def g_inside(lev, _):
         for b in range(W):
             g_col[lev, b] = weight_of(lev, b)
         return 0
 
-    lax.fori_loop(0, L // 2, g_inside, 0)
-    hear(0)
-    tell(1)
-    lax.fori_loop(L // 2, L, g_inside, 0)
+    lax.fori_loop(0, L, g_inside, 0)
 
     def departures(s, lev, first, count):
         w = [weight[tap, lev] for tap in range(4)]
@@ -290,8 +317,22 @@
         acc[S + s] = (totals[0] + totals[1]) + (totals[2] + totals[3])
         return 0
 
-    lax.fori_loop(0, S, inside, 0)
-
+    lax.fori_loop(0, S // 2, inside, 0)
+    hear(2)
+    tell(3)
+    lax.fori_loop(S // 2, S, inside, 0)
+
+    tile_up.wait_recv()
+    tile_down.wait_recv()
+
+    def relay_tiles(lev, _):
+        for l in range(ROWS):
+            rows = pl.ds(l, ROWS, stride=ROWS)
+            t_col[0, lev, LOW - ROWS + l] = t_halo[0, lev, rows, :]
+            t_col[0, lev, LOW + W + l] = t_halo[1, lev, rows, :]
+        return 0
+
+    lax.fori_loop(0, L, relay_tiles, 0)
     edge_up.wait_recv()
     edge_down.wait_recv()
     g_down.wait_recv()
@@ -328,9 +369,11 @@
 
     pair = remote(row_own, row_pair, pair_send.at[0], pair_recv.at[0], partner)
     pair.start()
+    hear(3)
+    tell(4)
     pair.wait_recv()
     row_chip[...] = row_own[...] + row_pair[...]
-    for r in range(1, rounds):
+    for r in range(4, rounds):
         hear(r)
         tell(r + 1)
 
@@ -350,32 +393,43 @@
     def near_from(side, d):
         return remote(row_chip, rows_near.at[side, d], near_send.at[0, d], near_recv.at[side, d], partner)
 
-    def cells(s, _):
-        bulk_up(s).wait_recv()
-        bulk_down(s).wait_recv()
-
-        def halo(lev, _):
-            for first in (-OFFMAX, -OFFMAX + 6, W, W + 6):
-                departures(s, lev, first, 6)
+    def halo(s, lev):
+        for first in (-OFFMAX, -OFFMAX + 6, W, W + 6):
+            departures(s, lev, first, 6)
+
+    def gather(s, lev, blk):
+        base = blk * ROWS
+        f = [f_col[s, lev, base + j] for j in range(ROWS + 2 * OFFMAX)]
+        for l in range(ROWS):
+            k = k_col[lev, base + l]
+            bits = [(k & (1 << bit)) != 0 for bit in range(5)]
+            out[s, lev, blk, pl.ds(l, ROWS, stride=ROWS), :] = pick(bits, f[l : l + 2 * OFFMAX + 1])
+
+    def level_cells(s, lev):
+        def part(blk, _):
+            gather(s, lev, blk)
             return 0
 
-        lax.fori_loop(0, L, halo, 0)
-
-        def gather(x, _):
-            lev, blk = x // blocks, lax.rem(x, blocks)
-            base = blk * ROWS
-            f = [f_col[s, lev, base + j] for j in range(ROWS + 2 * OFFMAX)]
-            for l in range(ROWS):
-                k = k_col[lev, base + l]
-                bits = [(k & (1 << bit)) != 0 for bit in range(5)]
-                out[s, lev, blk, pl.ds(l, ROWS, stride=ROWS), :] = pick(bits, f[l : l + 2 * OFFMAX + 1])
+        halo(s, lev)
+        lax.fori_loop(0, blocks, part, 0)
+
+    def cells(s, copies):
+        for copy in copies:
+            copy.wait_recv()
+
+        def level(lev, _):
+            level_cells(s, lev)
             return 0
 
-        lax.fori_loop(0, L * blocks, gather, 0)
-        return 0
-
-    early = S // 2 - 1
-    lax.fori_loop(0, early, cells, 0)
+        lax.fori_loop(0, L, level, 0)
+
+    def inner_cells(s, _):
+        cells(s, bulk_inner(s))
+        return 0
+
+    early = max(1, S // 2 - 1)
+    cells(0, bulk_first())
+    lax.fori_loop(1, early, inner_cells, 0)
 
     for side in range(2):
         for d in range(reach):
@@ -389,7 +443,11 @@
         copy.start()
     near_total = row_chip[...] + jnp.sum(rows_near[0], axis=0) + jnp.sum(rows_near[1], axis=0)
 
-    lax.fori_loop(early, S, cells, 0)
+    lax.fori_loop(early, S - 1, inner_cells, 0)
+    for lev in range(L):
+        for copy in bulk_last(lev):
+            copy.wait_recv()
+        level_cells(S - 1, lev)
 
     for side in range(2):
         remote(row_far_out, rows_far.at[side], far_send.at[0], far_recv.at[side], partner).wait_recv()
@@ -407,20 +465,18 @@
     for s in range(S):
         factor[s] = jnp.broadcast_to(ratio[s : s + 1, :], (ROWS, LANES))
 
-    edge_up.wait_send()
-    edge_down.wait_send()
-    g_down.wait_send()
-    g_up.wait_send()
-    pair.wait_send()
-    for copy in (*near, *far):
+    for copy in (tile_up, tile_down, edge_up, edge_down, g_down, g_up, pair, *near, *far, *bulk_first()):
         copy.wait_send()
+    for lev in range(L):
+        for copy in bulk_last(lev):
+            copy.wait_send()
 
     def finish(s, _):
-        bulk_up(s).wait_send()
-        bulk_down(s).wait_send()
-        return 0
-
-    lax.fori_loop(0, S, finish, 0)
+        for copy in bulk_inner(s):
+            copy.wait_send()
+        return 0
+
+    lax.fori_loop(1, S - 1, finish, 0)
 
 
 def scale_kernel(limited, factor, out, scaled, sem):
@@ -475,7 +531,7 @@
     blocks = W // ROWS
     dma = pltpu.SemaphoreType.DMA
     reach = n // 8
-    rounds = len(know_steps(min(NEAR, n // 2 - 1), 2 * reach + 1))
+    rounds = len(know_steps(1, 2 * reach + 1))
     small = (L, blocks, ROWS * ROWS, LANES)
     limited, factor = pl.pallas_call(
         functools.partial(kernel, (S, L, W, n)),
@@ -485,6 +541,7 @@
         out_specs=[pl.BlockSpec(memory_space=pltpu.VMEM)] * 2,
         scratch_shapes=[
             vmem(tiles.shape, f32),
+            vmem((2, L, ROWS * ROWS, LANES), f32),
             vmem(frac.shape, f32),
             pltpu.SMEM(growth.shape, f32),
             vmem(small, jnp.int32),
@@ -513,8 +570,10 @@
             dma((2,)),
             dma((2,)),
             dma((2,)),
-            dma((2, S)),
-            dma((2, S)),
+            dma((2,)),
+            dma((2,)),
+            dma((2, S - 1 + L)),
+            dma((2, S - 1 + L)),
             pltpu.SemaphoreType.REGULAR((rounds, 2)),
             dma((1,)),
             dma((1,)),

time: 53.2 us -> 50.9 us (0.957)
  Pallas kernels: 53.1 us -> 50.8 us
    pallas_call x1, Pallas kernels: 51 us -> 48.7 us  [on_device(): pl.pallas_call(functools.partial(kernel, (S, L, W, n)), out_shape=[pltpu....]
where the time goes in v4:
time: 50.9 us; the launch traced here: 50.8 us
  Pallas kernels  50.8 us (100%)
    pallas_call x1, Pallas kernels, on_device(): pl.pallas_call(functools.partial(kernel, (S, L, W, n)), out_shape=[pltpu....  48.7 us
    pallas_call x1, Pallas kernels, on_device(): pl.pallas_call(scale_kernel, out_shape=jax.ShapeDtypeStruct(tiles.shape,...  2.12 us

profile of v4, /device:TPU:37, one launch (start us, length us, event | category | flops | bytes accessed | tf_op | source)
XLA Modules:
  0.0 50.8 jit_solution(7588983278530077770)
XLA Ops:
  0.0 48.7 %shard_map.64 = (f32[8,4,4,64,128]{4,3,2,1,0:T(8,128)S(1)}, f32[8,8,128]{2,1,0:T(8,128)S(1)}) custom-call(f32[8,4,4,64,128]{4,3,2,1,0:T(8,128)} %bitcast.25, s32[4,4,64,128]{3,2,1,0:T(8,128)} %bitcast.26, f32[4,4,64,128]{3,2,1,0:T(8,128)} %bitcast.27, f32[4,4,64,128]{3,2,1,0:T(8,128)} %bitcast.28, f32[4,1024]{1,0:T(4,128)} %frac.1, f32[8]{0:T(128)} %growth.1), custom_call_target="tpu_custom_call" | custom-call | tf_op jit(solution)/shard_map/pallas_call | solution.py:536
  48.7 2.1 %shard_map.65 = f32[8,4,4,64,128]{4,3,2,1,0:T(8,128)} custom-call(f32[8,4,4,64,128]{4,3,2,1,0:T(8,128)S(1)} %get-tuple-element.7.limited, f32[8,8,128]{2,1,0:T(8,128)S(1)} %get-tuple-element.8.factor), custom_call_target="tpu_custom_call" | custom-call | tf_op jit(solution)/shard_map/pallas_call | solution.py:587

commit v5 on v4

--- a/solution.py
+++ b/solution.py
@@ -62,8 +62,10 @@
     ab_col,
     aa_col,
     g_col,
-    g_out,
-    g_halo,
+    g_out_down,
+    g_out_up,
+    g_low,
+    g_high,
     f_col,
     weight,
     acc,
@@ -133,15 +135,22 @@
 
     tile_up = remote(tracer.at[0, :, blocks - 1], t_halo.at[0], tile_send.at[0], tile_recv.at[0], right)
     tile_down = remote(tracer.at[0, :, 0], t_halo.at[1], tile_send.at[1], tile_recv.at[1], left)
-    others = pl.ds(1, S - 1)
-    edge_up = remote(
-        t_col.at[others, :, pl.ds(LOW + W - 1, 1)], t_col.at[others, :, pl.ds(LOW - 1, 1)], edge_send.at[0], edge_recv.at[0], right
-    )
-    edge_down = remote(
-        t_col.at[others, :, pl.ds(LOW, 2)], t_col.at[others, :, pl.ds(LOW + W, 2)], edge_send.at[1], edge_recv.at[1], left
-    )
-    g_down = remote(g_out.at[0], g_halo.at[1], g_send.at[0], g_recv.at[0], left)
-    g_up = remote(g_out.at[1], g_halo.at[0], g_send.at[1], g_recv.at[1], right)
+    half = S // 2
+
+    def edge(species, count, source, target, sem, to):
+        return remote(
+            t_col.at[species, :, pl.ds(source, count)], t_col.at[species, :, pl.ds(target, count)], edge_send.at[sem], edge_recv.at[sem], to
+        )
+
+    one_half, other_half = pl.ds(1, half - 1), pl.ds(half, S - half)
+    edges = [
+        edge(one_half, 2, LOW, LOW + W, 0, left),
+        edge(one_half, 1, LOW + W - 1, LOW - 1, 1, right),
+        edge(other_half, 2, LOW + W - 2, LOW - 2, 2, right),
+        edge(other_half, 1, LOW, LOW + W, 3, left),
+    ]
+    g_down = remote(g_out_down, g_high, g_send.at[0], g_recv.at[0], left)
+    g_up = remote(g_out_up, g_low, g_send.at[1], g_recv.at[1], right)
 
     def bulk(s, sem, levels, up_count, down_first):
         down_count = HIGH - down_first
@@ -165,11 +174,14 @@
     def bulk_first():
         return bulk(0, 0, pl.ds(0, L), LOW - ROWS, ROWS)
 
-    def bulk_inner(s):
+    def bulk_one(s):
         return bulk(s, s, pl.ds(0, L), LOW - 1, 2)
 
+    def bulk_other(s):
+        return bulk(s, s, pl.ds(0, L), LOW - 2, 1)
+
     def bulk_last(lev):
-        return bulk(S - 1, S - 1 + lev, pl.ds(lev, 1), LOW - 1, 2)
+        return bulk(S - 1, S - 1 + lev, pl.ds(lev, 1), LOW - 2, 1)
 
     steps = know_steps(1, 2 * reach + 1)
     rounds = len(steps)
@@ -196,13 +208,15 @@
 
     def relay_edges(s, _):
         for lev in range(L):
-            for blk, l in ((0, 0), (0, 1), (blocks - 1, ROWS - 1)):
+            for blk, l in ((0, 0), (0, 1), (blocks - 1, ROWS - 2), (blocks - 1, ROWS - 1)):
                 t_col[s, lev, LOW + blk * ROWS + l] = t_in[s, lev, blk, pl.ds(l, ROWS, stride=ROWS), :]
         return 0
 
     lax.fori_loop(0, S, relay_edges, 0)
-    edge_down.start()
-    edge_up.start()
+    for copy in edges:
+        copy.start()
+    hear(0)
+    tell(1)
     load_off.wait()
     load_aa.wait()
 
@@ -224,8 +238,9 @@
 
     def g_sides(lev, _):
         for j in range(OFFMAX):
-            g_out[0, lev, j] = weight_of(lev, j - OFFMAX)
-            g_out[1, lev, j] = weight_of(lev, W + j)
+            g_out_down[lev, j] = weight_of(lev, j - OFFMAX)
+        for j in range(OFFMAX + 1):
+            g_out_up[lev, j] = weight_of(lev, W - 1 + j)
         return 0
 
     lax.fori_loop(0, L, g_sides, 0)
@@ -237,8 +252,6 @@
             weight[tap, lev] = w
     g_down.start()
     g_up.start()
-    hear(0)
-    tell(1)
     load_ab.wait()
 
     def relay_before(x, _):
@@ -258,7 +271,7 @@
             totals = list(totals)
             for i in range(W):
                 blk, l = divmod(i, ROWS)
-                if 2 <= i < W - 1:
+                if 2 <= i < W - 2:
                     value = t_in[s, lev, blk, pl.ds(l, ROWS, stride=ROWS), :]
                     t_col[s, lev, LOW + i] = value
                 else:
@@ -270,28 +283,38 @@
         acc[s] = (totals[0] + totals[1]) + (totals[2] + totals[3])
         return 0
 
-    lax.fori_loop(0, S, relay_species, 0)
+    lax.fori_loop(0, half, relay_species, 0)
+    hear(1)
+    tell(2)
+    lax.fori_loop(half, S, relay_species, 0)
     for copy in bulk_first():
         copy.start()
 
-    def send_bulk(s, _):
-        for copy in bulk_inner(s):
+    def send_one(s, _):
+        for copy in bulk_one(s):
             copy.start()
         return 0
 
-    lax.fori_loop(1, S - 1, send_bulk, 0)
+    def send_other(s, _):
+        for copy in bulk_other(s):
+            copy.start()
+        return 0
+
+    lax.fori_loop(1, half, send_one, 0)
+    lax.fori_loop(half, S - 1, send_other, 0)
     for lev in range(L):
         for copy in bulk_last(lev):
             copy.start()
-    hear(1)
-    tell(2)
 
     def g_inside(lev, _):
-        for b in range(W):
+        for b in range(W - 1):
             g_col[lev, b] = weight_of(lev, b)
+        g_col[lev, W - 1] = g_out_up[lev, 0]
         return 0
 
     lax.fori_loop(0, L, g_inside, 0)
+    hear(2)
+    tell(3)
 
     def departures(s, lev, first, count):
         w = [weight[tap, lev] for tap in range(4)]
@@ -317,10 +340,9 @@
         acc[S + s] = (totals[0] + totals[1]) + (totals[2] + totals[3])
         return 0
 
-    lax.fori_loop(0, S // 2, inside, 0)
-    hear(2)
-    tell(3)
-    lax.fori_loop(S // 2, S, inside, 0)
+    lax.fori_loop(0, S, inside, 0)
+    hear(3)
+    tell(4)
 
     tile_up.wait_recv()
     tile_down.wait_recv()
@@ -333,28 +355,33 @@
         return 0
 
     lax.fori_loop(0, L, relay_tiles, 0)
-    edge_up.wait_recv()
-    edge_down.wait_recv()
+    for copy in edges:
+        copy.wait_recv()
     g_down.wait_recv()
     g_up.wait_recv()
 
     def outer_mass(lev, totals):
-        g_low = [g_halo[0, lev, j] for j in range(OFFMAX)]
-        g_high = [g_halo[1, lev, j] for j in range(OFFMAX)]
+        low = [g_low[lev, j] for j in range(OFFMAX + 1)]
+        high = [g_high[lev, j] for j in range(OFFMAX)]
+        low[0] = low[0] + g_out_down[lev, OFFMAX - 1]
+        low[1] = low[1] + g_col[lev, 0]
+        high[OFFMAX - 2] = high[OFFMAX - 2] + g_col[lev, W - 2]
+        high[OFFMAX - 1] = high[OFFMAX - 1] + g_col[lev, W - 1]
         sums = []
         for s in range(S):
             parts = [totals[s], zero]
-            (first,) = departures(s, lev, 0, 1)
-            last = departures(s, lev, W - 2, 2)
-            parts[0] = parts[0] + first * g_col[lev, 0]
-            parts[1] = parts[1] + last[0] * g_col[lev, W - 2]
-            parts[1] = parts[1] + last[1] * g_col[lev, W - 1]
-            for j in range(OFFMAX):
-                low = first if j == 0 else f_col[s, lev, OFFMAX + j]
-                at = W - OFFMAX + j
-                high = last[at - W + 2] if at >= W - 2 else f_col[s, lev, OFFMAX + at]
-                parts[0] = parts[0] + low * g_low[j]
-                parts[1] = parts[1] + high * g_high[j]
+            if s < half:
+                first, last = departures(s, lev, 0, 1), departures(s, lev, W - 2, 2)
+            else:
+                first, last = departures(s, lev, -1, 2), departures(s, lev, W - 2, 1)
+            near_low = [(first[-1], low[1])] + [(f_col[s, lev, OFFMAX + j], low[1 + j]) for j in range(1, OFFMAX)]
+            if s >= half:
+                near_low.append((first[0], low[0]))
+            near_high = [(f_col[s, lev, W + j], high[j]) for j in range(OFFMAX - 2)]
+            near_high += [(value, high[OFFMAX - 2 + j]) for j, value in enumerate(last)]
+            for i, pairs in enumerate((near_low, near_high)):
+                for value, mass in pairs:
+                    parts[i] = parts[i] + value * mass
             sums.append(parts[0] + parts[1])
         return tuple(sums)
 
@@ -369,8 +396,6 @@
 
     pair = remote(row_own, row_pair, pair_send.at[0], pair_recv.at[0], partner)
     pair.start()
-    hear(3)
-    tell(4)
     pair.wait_recv()
     row_chip[...] = row_own[...] + row_pair[...]
     for r in range(4, rounds):
@@ -383,19 +408,24 @@
         return away(way * d - core + at)
 
     near = [
-        remote(row_chip, rows_near.at[core, d], near_send.at[at, d], near_recv.at[core, d], to_chip(d + 1, at))
+        [remote(row_chip, rows_near.at[core, d], near_send.at[at, d], near_recv.at[core, d], to_chip(d + 1, at)) for at in range(2)]
         for d in range(reach)
-        for at in range(2)
     ]
-    for copy in near:
-        copy.start()
+    for d in range(reach - 1):
+        for copy in near[d]:
+            copy.start()
+
+    @pl.when(core == 1)
+    def _():
+        for copy in near[reach - 1]:
+            copy.start()
 
     def near_from(side, d):
         return remote(row_chip, rows_near.at[side, d], near_send.at[0, d], near_recv.at[side, d], partner)
 
     def halo(s, lev):
-        for first in (-OFFMAX, -OFFMAX + 6, W, W + 6):
-            departures(s, lev, first, 6)
+        for first, count in ((-OFFMAX, 6), (-OFFMAX + 6, 6), (W - 1, 7), (W + 6, 6)):
+            departures(s, lev, first, count)
 
     def gather(s, lev, blk):
         base = blk * ROWS
@@ -423,27 +453,47 @@
 
         lax.fori_loop(0, L, level, 0)
 
-    def inner_cells(s, _):
-        cells(s, bulk_inner(s))
-        return 0
-
-    early = max(1, S // 2 - 1)
+    def one_cells(s, _):
+        cells(s, bulk_one(s))
+        return 0
+
+    def other_cells(s, _):
+        cells(s, bulk_other(s))
+        return 0
+
+    early = max(1, half - 1)
     cells(0, bulk_first())
-    lax.fori_loop(1, early, inner_cells, 0)
-
-    for side in range(2):
-        for d in range(reach):
-            near_from(side, d).wait_recv()
+    lax.fori_loop(1, early, one_cells, 0)
+
+    for d in range(reach - 1):
+        near_from(core, d).wait_recv()
     mine = jnp.sum(rows_near[core, pl.ds(0, reach - 1)], axis=0)
-    row_far_out[...] = mine + jnp.where(core == 0, 1.0, 0.0) * rows_near[core, reach - 1]
+
+    @pl.when(core == 0)
+    def _():
+        row_far_out[...] = mine + row_chip[...]
+
+    @pl.when(core == 1)
+    def _():
+        near_from(1, reach - 1).wait_recv()
+        row_far_out[...] = mine + rows_near[1, reach - 1]
+
     far = [
         remote(row_far_out, rows_far.at[core], far_send.at[at], far_recv.at[core], to_chip(reach, at)) for at in range(2)
     ]
     for copy in far:
         copy.start()
-    near_total = row_chip[...] + jnp.sum(rows_near[0], axis=0) + jnp.sum(rows_near[1], axis=0)
-
-    lax.fori_loop(early, S - 1, inner_cells, 0)
+    for d in range(reach - 1):
+        near_from(1 - core, d).wait_recv()
+
+    @pl.when(core == 0)
+    def _():
+        near_from(1, reach - 1).wait_recv()
+
+    near_total = row_chip[...] + jnp.sum(rows_near[0, pl.ds(0, reach - 1)], axis=0) + jnp.sum(rows_near[1], axis=0)
+
+    lax.fori_loop(early, half, one_cells, 0)
+    lax.fori_loop(half, S - 1, other_cells, 0)
     for lev in range(L):
         for copy in bulk_last(lev):
             copy.wait_recv()
@@ -465,18 +515,30 @@
     for s in range(S):
         factor[s] = jnp.broadcast_to(ratio[s : s + 1, :], (ROWS, LANES))
 
-    for copy in (tile_up, tile_down, edge_up, edge_down, g_down, g_up, pair, *near, *far, *bulk_first()):
+    for copy in (tile_up, tile_down, *edges, g_down, g_up, pair, *sum(near[:-1], []), *far, *bulk_first()):
         copy.wait_send()
+
+    @pl.when(core == 1)
+    def _():
+        for copy in near[reach - 1]:
+            copy.wait_send()
+
     for lev in range(L):
         for copy in bulk_last(lev):
             copy.wait_send()
 
-    def finish(s, _):
-        for copy in bulk_inner(s):
+    def finish_one(s, _):
+        for copy in bulk_one(s):
             copy.wait_send()
         return 0
 
-    lax.fori_loop(1, S - 1, finish, 0)
+    def finish_other(s, _):
+        for copy in bulk_other(s):
+            copy.wait_send()
+        return 0
+
+    lax.fori_loop(1, half, finish_one, 0)
+    lax.fori_loop(half, S - 1, finish_other, 0)
 
 
 def scale_kernel(limited, factor, out, scaled, sem):
@@ -552,8 +614,10 @@
             vmem((L, W, *column), f32),
             vmem((L, W, *column), f32),
             vmem((L, W, *column), f32),
-            vmem((2, L, OFFMAX, *column), f32),
-            vmem((2, L, OFFMAX, *column), f32),
+            vmem((L, OFFMAX, *column), f32),
+            vmem((L, OFFMAX + 1, *column), f32),
+            vmem((L, OFFMAX + 1, *column), f32),
+            vmem((L, OFFMAX, *column), f32),
             vmem((S, L, W + 2 * OFFMAX, *column), f32),
             vmem((4, L, *column), f32),
             vmem((2 * S, *column), f32),
@@ -568,8 +632,8 @@
             dma((5,)),
             dma((2,)),
             dma((2,)),
-            dma((2,)),
-            dma((2,)),
+            dma((4,)),
+            dma((4,)),
             dma((2,)),
             dma((2,)),
             dma((2, S - 1 + L)),

time: 50.9 us -> 49.4 us (0.971)
  Pallas kernels: 50.8 us -> 48.9 us
    pallas_call x1, Pallas kernels: 48.7 us -> 46.8 us  [on_device(): pl.pallas_call(functools.partial(kernel, (S, L, W, n)), out_shape=[pltpu....]
where the time goes in v5:
time: 49.4 us; the launch traced here: 48.9 us
  Pallas kernels  48.9 us (99%)
    pallas_call x1, Pallas kernels, on_device(): pl.pallas_call(functools.partial(kernel, (S, L, W, n)), out_shape=[pltpu....  46.8 us
    pallas_call x1, Pallas kernels, on_device(): pl.pallas_call(scale_kernel, out_shape=jax.ShapeDtypeStruct(tiles.shape,...  2.12 us

profile of v5, /device:TPU:37, one launch (start us, length us, event | category | flops | bytes accessed | tf_op | source)
XLA Modules:
  0.0 48.9 jit_solution(1816400119465007030)
XLA Ops:
  0.0 46.8 %shard_map.64 = (f32[8,4,4,64,128]{4,3,2,1,0:T(8,128)S(1)}, f32[8,8,128]{2,1,0:T(8,128)S(1)}) custom-call(f32[8,4,4,64,128]{4,3,2,1,0:T(8,128)} %bitcast.25, s32[4,4,64,128]{3,2,1,0:T(8,128)} %bitcast.26, f32[4,4,64,128]{3,2,1,0:T(8,128)} %bitcast.27, f32[4,4,64,128]{3,2,1,0:T(8,128)} %bitcast.28, f32[4,1024]{1,0:T(4,128)} %frac.1, f32[8]{0:T(128)} %growth.1), custom_call_target="tpu_custom_call" | custom-call | tf_op jit(solution)/shard_map/pallas_call | solution.py:598
  46.8 2.1 %shard_map.65 = f32[8,4,4,64,128]{4,3,2,1,0:T(8,128)} custom-call(f32[8,4,4,64,128]{4,3,2,1,0:T(8,128)S(1)} %get-tuple-element.7.limited, f32[8,8,128]{2,1,0:T(8,128)S(1)} %get-tuple-element.8.factor), custom_call_target="tpu_custom_call" | custom-call | tf_op jit(solution)/shard_map/pallas_call | solution.py:651

commit v6 on v5

--- a/solution.py
+++ b/solution.py
@@ -73,6 +73,8 @@
     row_pair,
     row_chip,
     rows_near,
+    row_side,
+    row_other,
     row_far_out,
     rows_far,
     edge_in_sem,
@@ -403,25 +405,14 @@
         tell(r + 1)
 
     way = 2 * (1 - 2 * core)
-
-    def to_chip(d, at):
-        return away(way * d - core + at)
-
-    near = [
-        [remote(row_chip, rows_near.at[core, d], near_send.at[at, d], near_recv.at[core, d], to_chip(d + 1, at)) for at in range(2)]
-        for d in range(reach)
-    ]
-    for d in range(reach - 1):
-        for copy in near[d]:
-            copy.start()
+    near = [remote(row_chip, rows_near.at[d], near_send.at[d], near_recv.at[d], away(way * (d + 1))) for d in range(reach)]
 
     @pl.when(core == 1)
     def _():
-        for copy in near[reach - 1]:
-            copy.start()
-
-    def near_from(side, d):
-        return remote(row_chip, rows_near.at[side, d], near_send.at[0, d], near_recv.at[side, d], partner)
+        near[reach - 1].start()
+
+    for copy in near[reach - 2 :: -1]:
+        copy.start()
 
     def halo(s, lev):
         for first, count in ((-OFFMAX, 6), (-OFFMAX + 6, 6), (W - 1, 7), (W + 6, 6)):
@@ -465,44 +456,43 @@
     cells(0, bulk_first())
     lax.fori_loop(1, early, one_cells, 0)
 
-    for d in range(reach - 1):
-        near_from(core, d).wait_recv()
-    mine = jnp.sum(rows_near[core, pl.ds(0, reach - 1)], axis=0)
+    for copy in near[:-1]:
+        copy.wait_recv()
+    mine = jnp.sum(rows_near[pl.ds(0, reach - 1)], axis=0)
 
     @pl.when(core == 0)
     def _():
         row_far_out[...] = mine + row_chip[...]
+        row_side[...] = mine
 
     @pl.when(core == 1)
     def _():
-        near_from(1, reach - 1).wait_recv()
-        row_far_out[...] = mine + rows_near[1, reach - 1]
+        near[reach - 1].wait_recv()
+        row_far_out[...] = mine + rows_near[reach - 1]
+        row_side[...] = mine + rows_near[reach - 1]
 
     far = [
-        remote(row_far_out, rows_far.at[core], far_send.at[at], far_recv.at[core], to_chip(reach, at)) for at in range(2)
+        remote(row_far_out, rows_far.at[core], far_send.at[at], far_recv.at[core], away(way * reach - core + at)) for at in range(2)
     ]
     for copy in far:
         copy.start()
-    for d in range(reach - 1):
-        near_from(1 - core, d).wait_recv()
-
-    @pl.when(core == 0)
-    def _():
-        near_from(1, reach - 1).wait_recv()
-
-    near_total = row_chip[...] + jnp.sum(rows_near[0, pl.ds(0, reach - 1)], axis=0) + jnp.sum(rows_near[1], axis=0)
+    swap = remote(row_side, row_other, pair_send.at[1], pair_recv.at[1], partner)
+    swap.start()
 
     lax.fori_loop(early, half, one_cells, 0)
     lax.fori_loop(half, S - 1, other_cells, 0)
-    for lev in range(L):
+    def last_cells(lev):
         for copy in bulk_last(lev):
             copy.wait_recv()
         level_cells(S - 1, lev)
 
+    for lev in range(L - 1):
+        last_cells(lev)
+    swap.wait_recv()
     for side in range(2):
         remote(row_far_out, rows_far.at[side], far_send.at[0], far_recv.at[side], partner).wait_recv()
     load_growth.wait()
-    total = near_total + (rows_far[0] + rows_far[1])
+    total = row_chip[...] + (row_side[...] + row_other[...]) + (rows_far[0] + rows_far[1])
     spread = jnp.broadcast_to(total, (S, LANES))
     at_row = lax.broadcasted_iota(jnp.int32, (S, LANES), 0)
     at_lane = lax.broadcasted_iota(jnp.int32, (S, LANES), 1)
@@ -515,13 +505,14 @@
     for s in range(S):
         factor[s] = jnp.broadcast_to(ratio[s : s + 1, :], (ROWS, LANES))
 
-    for copy in (tile_up, tile_down, *edges, g_down, g_up, pair, *sum(near[:-1], []), *far, *bulk_first()):
+    last_cells(L - 1)
+
+    for copy in (tile_up, tile_down, *edges, g_down, g_up, pair, swap, *near[:-1], *far, *bulk_first()):
         copy.wait_send()
 
     @pl.when(core == 1)
     def _():
-        for copy in near[reach - 1]:
-            copy.wait_send()
+        near[reach - 1].wait_send()
 
     for lev in range(L):
         for copy in bulk_last(lev):
@@ -624,7 +615,9 @@
             vmem((1, LANES), f32),
             vmem((1, LANES), f32),
             vmem((1, LANES), f32),
-            vmem((2, reach, 1, LANES), f32),
+            vmem((reach, 1, LANES), f32),
+            vmem((1, LANES), f32),
+            vmem((1, LANES), f32),
             vmem((1, LANES), f32),
             vmem((2, 1, LANES), f32),
             dma((2,)),
@@ -639,10 +632,10 @@
             dma((2, S - 1 + L)),
             dma((2, S - 1 + L)),
             pltpu.SemaphoreType.REGULAR((rounds, 2)),
-            dma((1,)),
-            dma((1,)),
-            dma((2, reach)),
-            dma((2, reach)),
+            dma((2,)),
+            dma((2,)),
+            dma((reach,)),
+            dma((reach,)),
             dma((2,)),
             dma((2,)),
         ],

time: 49.4 us -> 49.1 us (level)
  no operation moved by 1% of the time
where the time goes in v6:
time: 49.1 us; the launch traced here: 48.5 us
  Pallas kernels  48.5 us (99%)
    pallas_call x1, Pallas kernels, on_device(): pl.pallas_call(functools.partial(kernel, (S, L, W, n)), out_shape=[pltpu....  46.3 us
    pallas_call x1, Pallas kernels, on_device(): pl.pallas_call(scale_kernel, out_shape=jax.ShapeDtypeStruct(tiles.shape,...  2.12 us

profile of v6, /device:TPU:37, one launch (start us, length us, event | category | flops | bytes accessed | tf_op | source)
XLA Modules:
  0.0 48.5 jit_solution(14836439587611290244)
XLA Ops:
  0.0 46.3 %shard_map.64 = (f32[8,4,4,64,128]{4,3,2,1,0:T(8,128)S(1)}, f32[8,8,128]{2,1,0:T(8,128)S(1)}) custom-call(f32[8,4,4,64,128]{4,3,2,1,0:T(8,128)} %bitcast.25, s32[4,4,64,128]{3,2,1,0:T(8,128)} %bitcast.26, f32[4,4,64,128]{3,2,1,0:T(8,128)} %bitcast.27, f32[4,4,64,128]{3,2,1,0:T(8,128)} %bitcast.28, f32[4,1024]{1,0:T(4,128)} %frac.1, f32[8]{0:T(128)} %growth.1), custom_call_target="tpu_custom_call" | custom-call | tf_op jit(solution)/shard_map/pallas_call | solution.py:589
  46.4 2.1 %shard_map.65 = f32[8,4,4,64,128]{4,3,2,1,0:T(8,128)} custom-call(f32[8,4,4,64,128]{4,3,2,1,0:T(8,128)S(1)} %get-tuple-element.7.limited, f32[8,8,128]{2,1,0:T(8,128)S(1)} %get-tuple-element.8.factor), custom_call_target="tpu_custom_call" | custom-call | tf_op jit(solution)/shard_map/pallas_call | solution.py:644

commit v7 on v6

--- a/solution.py
+++ b/solution.py
@@ -49,7 +49,6 @@
     frac,
     growth,
     out,
-    factor,
     t_in,
     t_halo,
     frac_in,
@@ -69,6 +68,7 @@
     f_col,
     weight,
     acc,
+    factor,
     row_own,
     row_pair,
     row_chip,
@@ -505,7 +505,17 @@
     for s in range(S):
         factor[s] = jnp.broadcast_to(ratio[s : s + 1, :], (ROWS, LANES))
 
+    def scale(x, _):
+        s, lev = x // L, lax.rem(x, L)
+        gain = factor[s]
+        for blk in range(blocks):
+            for row in range(0, out.shape[3], ROWS):
+                out[s, lev, blk, pl.ds(row, ROWS), :] = out[s, lev, blk, pl.ds(row, ROWS), :] * gain
+        return 0
+
+    lax.fori_loop(0, S * L - 1, scale, 0)
     last_cells(L - 1)
+    scale(S * L - 1, 0)
 
     for copy in (tile_up, tile_down, *edges, g_down, g_up, pair, swap, *near[:-1], *far, *bulk_first()):
         copy.wait_send()
@@ -532,27 +542,13 @@
     lax.fori_loop(half, S - 1, finish_other, 0)
 
 
-def scale_kernel(limited, factor, out, scaled, sem):
-    S, L = limited.shape[:2]
-
+def write_kernel(scaled, out, sem):
     def put(s):
         return pltpu.make_async_copy(scaled.at[s], out.at[s], sem.at[s])
 
-    def scale(s, _):
-        gain = factor[s]
-
-        def level(lev, _):
-            for blk in range(limited.shape[2]):
-                for row in range(0, limited.shape[3], ROWS):
-                    scaled[s, lev, blk, pl.ds(row, ROWS), :] = limited[s, lev, blk, pl.ds(row, ROWS), :] * gain
-            return 0
-
-        lax.fori_loop(0, L, level, 0)
+    for s in range(out.shape[0]):
         put(s).start()
-        return 0
-
-    lax.fori_loop(0, S, scale, 0)
-    for s in range(S):
+    for s in range(out.shape[0]):
         put(s).wait()
 
 
@@ -586,12 +582,12 @@
     reach = n // 8
     rounds = len(know_steps(1, 2 * reach + 1))
     small = (L, blocks, ROWS * ROWS, LANES)
-    limited, factor = pl.pallas_call(
+    scaled = pl.pallas_call(
         functools.partial(kernel, (S, L, W, n)),
-        out_shape=[pltpu.VMEM(tiles.shape, f32), pltpu.VMEM((S, *column), f32)],
+        out_shape=pltpu.VMEM(tiles.shape, f32),
         in_specs=[pl.BlockSpec(memory_space=pltpu.HBM)] * 6,
 
-        out_specs=[pl.BlockSpec(memory_space=pltpu.VMEM)] * 2,
+        out_specs=pl.BlockSpec(memory_space=pltpu.VMEM),
         scratch_shapes=[
             vmem(tiles.shape, f32),
             vmem((2, L, ROWS * ROWS, LANES), f32),
@@ -612,6 +608,7 @@
             vmem((S, L, W + 2 * OFFMAX, *column), f32),
             vmem((4, L, *column), f32),
             vmem((2 * S, *column), f32),
+            vmem((S, *column), f32),
             vmem((1, LANES), f32),
             vmem((1, LANES), f32),
             vmem((1, LANES), f32),
@@ -642,13 +639,13 @@
         compiler_params=pltpu.CompilerParams(collective_id=0, has_side_effects=True, vmem_limit_bytes=44 * 2**20),
     )(*map(in_hbm, (tiles, to_tiles(offsets), to_tiles(air_before), to_tiles(air_after), frac, growth)))
     result = pl.pallas_call(
-        scale_kernel,
+        write_kernel,
         out_shape=jax.ShapeDtypeStruct(tiles.shape, f32),
-        in_specs=[pl.BlockSpec(memory_space=pltpu.VMEM)] * 2,
+        in_specs=[pl.BlockSpec(memory_space=pltpu.VMEM)],
         out_specs=pl.BlockSpec(memory_space=pl.ANY),
-        scratch_shapes=[vmem(tiles.shape, f32), dma((S,))],
+        scratch_shapes=[dma((S,))],
         compiler_params=pltpu.CompilerParams(vmem_limit_bytes=24 * 2**20),
-    )(limited, factor)
+    )(scaled)
     return from_tiles(result, W, lats)
 
 

time: 49.1 us -> 49.2 us (level)
  Pallas kernels: 48.5 us -> 49 us
    pallas_call x2, Pallas kernels: 48.5 us -> 49 us  [the longest x1 46.9 us: on_device(): pl.pallas_call(functools.partial(kernel, (S, L, W, n)), out_shape=pltpu.V...]
where the time goes in v7:
time: 49.2 us; the launch traced here: 49 us
  Pallas kernels  49 us (100%)
    pallas_call x1, Pallas kernels, on_device(): pl.pallas_call(functools.partial(kernel, (S, L, W, n)), out_shape=pltpu.V...  46.9 us
    pallas_call x1, Pallas kernels, on_device(): pl.pallas_call(write_kernel, out_shape=jax.ShapeDtypeStruct(tiles.shape,...  2.07 us

profile of v7, /device:TPU:37, one launch (start us, length us, event | category | flops | bytes accessed | tf_op | source)
XLA Modules:
  0.0 49.0 jit_solution(9990494877843414375)
XLA Ops:
  0.0 46.9 %shard_map.64.scaled = f32[8,4,4,64,128]{4,3,2,1,0:T(8,128)S(1)} custom-call(f32[8,4,4,64,128]{4,3,2,1,0:T(8,128)} %bitcast.25, s32[4,4,64,128]{3,2,1,0:T(8,128)} %bitcast.26, f32[4,4,64,128]{3,2,1,0:T(8,128)} %bitcast.27, f32[4,4,64,128]{3,2,1,0:T(8,128)} %bitcast.28, f32[4,1024]{1,0:T(4,128)} %frac.1, f32[8]{0:T(128)} %growth.1), custom_call_target="tpu_custom_call" | custom-call | tf_op jit(solution)/shard_map/pallas_call | solution.py:585
  46.9 2.1 %shard_map.65 = f32[8,4,4,64,128]{4,3,2,1,0:T(8,128)} custom-call(f32[8,4,4,64,128]{4,3,2,1,0:T(8,128)S(1)} %shard_map.64.scaled), custom_call_target="tpu_custom_call" | custom-call | tf_op jit(solution)/shard_map/pallas_call | solution.py:641

commit v8 on v6

--- a/solution.py
+++ b/solution.py
@@ -535,25 +535,24 @@
 def scale_kernel(limited, factor, out, scaled, sem):
     S, L = limited.shape[:2]
 
-    def put(s):
-        return pltpu.make_async_copy(scaled.at[s], out.at[s], sem.at[s])
-
-    def scale(s, _):
+    def put(s, lev):
+        return pltpu.make_async_copy(scaled.at[s, lev], out.at[s, lev], sem.at[s, lev])
+
+    def scale(x, _):
+        s, lev = x // L, lax.rem(x, L)
         gain = factor[s]
-
-        def level(lev, _):
-            for blk in range(limited.shape[2]):
-                for row in range(0, limited.shape[3], ROWS):
-                    scaled[s, lev, blk, pl.ds(row, ROWS), :] = limited[s, lev, blk, pl.ds(row, ROWS), :] * gain
-            return 0
-
-        lax.fori_loop(0, L, level, 0)
-        put(s).start()
-        return 0
-
-    lax.fori_loop(0, S, scale, 0)
-    for s in range(S):
-        put(s).wait()
+        for blk in range(limited.shape[2]):
+            for row in range(0, limited.shape[3], ROWS):
+                scaled[s, lev, blk, pl.ds(row, ROWS), :] = limited[s, lev, blk, pl.ds(row, ROWS), :] * gain
+        put(s, lev).start()
+        return 0
+
+    def finish(x, _):
+        put(x // L, lax.rem(x, L)).wait()
+        return 0
+
+    lax.fori_loop(0, S * L, scale, 0)
+    lax.fori_loop(0, S * L, finish, 0)
 
 
 def to_tiles(a):
@@ -646,7 +645,7 @@
         out_shape=jax.ShapeDtypeStruct(tiles.shape, f32),
         in_specs=[pl.BlockSpec(memory_space=pltpu.VMEM)] * 2,
         out_specs=pl.BlockSpec(memory_space=pl.ANY),
-        scratch_shapes=[vmem(tiles.shape, f32), dma((S,))],
+        scratch_shapes=[vmem(tiles.shape, f32), dma((S, L))],
         compiler_params=pltpu.CompilerParams(vmem_limit_bytes=24 * 2**20),
     )(limited, factor)
     return from_tiles(result, W, lats)

time: 49.1 us -> 49.3 us (level)
  no operation moved by 1% of the time
where the time goes in v8:
time: 49.3 us; the launch traced here: 48.6 us
  Pallas kernels  48.6 us (99%)
    pallas_call x1, Pallas kernels, on_device(): pl.pallas_call(functools.partial(kernel, (S, L, W, n)), out_shape=[pltpu....  46.3 us
    pallas_call x1, Pallas kernels, on_device(): pl.pallas_call(scale_kernel, out_shape=jax.ShapeDtypeStruct(tiles.shape,...  2.28 us

profile of v8, /device:TPU:37, one launch (start us, length us, event | category | flops | bytes accessed | tf_op | source)
XLA Modules:
  0.0 48.6 jit_solution(3958426103904650483)
XLA Ops:
  0.0 46.3 %shard_map.64 = (f32[8,4,4,64,128]{4,3,2,1,0:T(8,128)S(1)}, f32[8,8,128]{2,1,0:T(8,128)S(1)}) custom-call(f32[8,4,4,64,128]{4,3,2,1,0:T(8,128)} %bitcast.25, s32[4,4,64,128]{3,2,1,0:T(8,128)} %bitcast.26, f32[4,4,64,128]{3,2,1,0:T(8,128)} %bitcast.27, f32[4,4,64,128]{3,2,1,0:T(8,128)} %bitcast.28, f32[4,1024]{1,0:T(4,128)} %frac.1, f32[8]{0:T(128)} %growth.1), custom_call_target="tpu_custom_call" | custom-call | tf_op jit(solution)/shard_map/pallas_call | solution.py:588
  46.4 2.3 %shard_map.65 = f32[8,4,4,64,128]{4,3,2,1,0:T(8,128)} custom-call(f32[8,4,4,64,128]{4,3,2,1,0:T(8,128)S(1)} %get-tuple-element.7.limited, f32[8,8,128]{2,1,0:T(8,128)S(1)} %get-tuple-element.8.factor), custom_call_target="tpu_custom_call" | custom-call | tf_op jit(solution)/shard_map/pallas_call | solution.py:643
